TPU v7x, 128 devices: a whole 4x4x4 slice. The times are simulated.
128 devices in a mesh: batch: 8 (over x_lo, y), mp: 16 (over x_hi, z, core).
Axes of the slice: x: 4 (x_hi: 2, x_lo: 2; x = x_hi * 2 + x_lo), y: 4, z: 4, core: 2. Of those that a mesh axis runs over, the one named last changes fastest.
Arguments:
- pixels: bfloat16 [8, 16, 8, 100, 768], P('batch', 'mp'), may hold values from -6 to 6
- patch_weight: bfloat16 [768, 1024], P('mp'), may hold values from -0.21875 to 0.21875
- position: bfloat16 [100, 1024], replicated, may hold values from -3 to 3
- encoder_gains: float32 [3, 1024], replicated, may hold values from 0.25 to 1.75
- qkv_weight: bfloat16 [1024, 3072], P('mp'), may hold values from -0.1875 to 0.1875
- out_weight: bfloat16 [1024, 1024], P('mp'), may hold values from -0.1875 to 0.1875
- up_weight: bfloat16 [1024, 4096], P('mp'), may hold values from -0.1875 to 0.1875
- down_weight: bfloat16 [4096, 1024], P('mp'), may hold values from -0.09375 to 0.09375
- cond_weight: bfloat16 [1024, 512], replicated, may hold values from -0.1875 to 0.1875
- time_weight: float32 [512, 512], replicated, may hold values from -0.5 to 0.5
- action_in: float32 [10, 512], replicated, may hold values from -2 to 2
- action_pos: float32 [16, 512], replicated, may hold values from -3 to 3
- denoise_gains: float32 [3, 512], replicated, may hold values from 0.25 to 1.75
- self_qkv: bfloat16 [512, 1536], replicated, may hold values from -0.25 to 0.25
- self_out: bfloat16 [512, 512], replicated, may hold values from -0.25 to 0.25
- cross_query: bfloat16 [512, 512], replicated, may hold values from -0.25 to 0.25
- cross_kv: bfloat16 [512, 1024], replicated, may hold values from -0.25 to 0.25
- cross_out: bfloat16 [512, 512], replicated, may hold values from -0.25 to 0.25
- mix_up: bfloat16 [512, 2048], replicated, may hold values from -0.25 to 0.25
- mix_down: bfloat16 [2048, 512], replicated, may hold values from -0.125 to 0.125
- action_out: float32 [512, 10], replicated, may hold values from -0.25 to 0.25
- noise: float32 [16, 8, 8, 16, 10], P('mp', 'batch'), may hold values from -5 to 5
- timesteps: int32 [4], replicated, may hold values from 5 to 79, as said below
Outputs:
- actions: float32 [16, 8, 8, 16, 10], P('mp', 'batch')
Inputs may be any that keep to these rules, and one draw needn't show every extreme that they name: `timesteps`: strictly decreasing.
All inputs are finite; a program needn't handle non-finite values.
Results may differ from a plain program's by a relative error of at most 0.0033.
Values may be sent and summed in bfloat16 or wider, within the bound.
A program may use at most 192 MiB of HBM per device.

v0:
```python
import math

import jax
import jax.numpy as jnp
from jax import lax
from jax.experimental import pallas as pl
from jax.experimental.pallas import tpu as pltpu
from jax.sharding import PartitionSpec as P

HEADS = 16
GRID = 10
DHEADS = 8
STEPS = 4
TMAX = 100


norm_eps = 1e-06
offset = 0.008


def in_one_piece(arrays, axis, dim, along):
    widths = [a.shape[along] for a in arrays]
    both = jnp.concatenate(arrays, axis=along)
    result = lax.all_gather(both, axis, axis=dim, tiled=True)
    return tuple(jnp.split(result, [sum(widths[:k]) for k in range(1, len(widths))], axis=along))


def normalize(values, gain):
    middle = jnp.mean(values, -1, keepdims=True)
    centred = values - middle
    spread = jnp.mean(centred * centred, -1, keepdims=True)
    return centred * lax.rsqrt(spread + norm_eps) * gain


def plan(level):
    angle = (level.astype(jnp.float32) / TMAX + offset) / (1.0 + offset) * (math.pi / 2)
    base = math.cos(offset / (1.0 + offset) * math.pi / 2) ** 2
    return jnp.cos(angle) ** 2 / base


def product(left, right):
    return jnp.dot(left, right, preferred_element_type=jnp.float32)


def precise(left, right):
    return jnp.dot(left, right, precision=lax.Precision.HIGHEST)


def contract(form, left, right):
    return jnp.einsum(form, left, right, preferred_element_type=jnp.float32)


VMEM = pltpu.VMEM
KEYS = 32


def stacked_heads(block):
    lane = lax.broadcasted_iota(jnp.int32, block.shape, 1)
    low = jnp.where(lane < 64, block, jnp.zeros_like(block))
    high = jnp.where(lane < 64, jnp.zeros_like(block), block)
    return jnp.concatenate([low, high], axis=0)


def pair_attention(query, keys, values, allowed):
    rows = query.shape[0]
    scores = lax.dot_general(
        stacked_heads(query), keys, (((1,), (1,)), ((), ())), preferred_element_type=jnp.float32
    )
    scores = jnp.where(allowed, scores * 0.125, -1e30)
    top = jnp.max(scores, axis=-1, keepdims=True)
    grown = jnp.exp(scores - top)
    probs = (grown / jnp.sum(grown, axis=-1, keepdims=True)).astype(jnp.bfloat16)
    both = jnp.dot(probs, values, preferred_element_type=jnp.float32)
    lane = lax.broadcasted_iota(jnp.int32, (rows, 128), 1)
    return jnp.where(lane < 64, both[:rows], both[rows:]).astype(jnp.bfloat16)


def gelu(values):
    return 0.5 * values * (1.0 + lax.erf(values * math.sqrt(0.5)))


def denoise_kernel(
    levels_ref,
    noise_ref,
    condition_ref,
    time_ref,
    in_ref,
    pos_ref,
    gains_ref,
    qkv_ref,
    self_out_ref,
    query_ref,
    kv_ref,
    cross_out_ref,
    up_ref,
    down_ref,
    out_ref,
    actions_ref,
    memory,
    stamps,
    packed,
    context,
):
    width = 512
    rows = 128
    memory[...] = product(condition_ref[...], kv_ref[...]).astype(jnp.bfloat16)
    row = lax.broadcasted_iota(jnp.int32, (8, width // 2), 0)
    level = jnp.zeros((8, width // 2), jnp.float32)
    for step in range(STEPS):
        level = jnp.where(row == step, levels_ref[step].astype(jnp.float32), level)
    order = lax.broadcasted_iota(jnp.int32, (8, width // 2), 1).astype(jnp.float32)
    phase = level * jnp.exp(order * (-math.log(10000.0) / (width // 2)))
    waves = jnp.concatenate([jnp.sin(phase), jnp.cos(phase)], axis=1)
    stamps[...] = precise(waves, time_ref[...])
    actions_ref[...] = noise_ref[...]

    own = lax.broadcasted_iota(jnp.int32, (2 * rows, rows), 0)
    other = lax.broadcasted_iota(jnp.int32, (2 * rows, rows), 1)
    same = lax.rem(own, rows) // 16 == other // 16
    slot = lax.broadcasted_iota(jnp.int32, (2 * rows, 8 * KEYS), 1)
    held = lax.rem(slot, KEYS) < 25

    def one_step(step, carry):
        sample = actions_ref[...]
        state = precise(sample, in_ref[...])
        state = (state.reshape(8, 16, width) + pos_ref[...]).reshape(rows, width)
        state = state + stamps[pl.ds(step, 1), :]
        normed = normalize(state, gains_ref[0:1, :]).astype(jnp.bfloat16)
        packed[...] = product(normed, qkv_ref[...]).astype(jnp.bfloat16)
        for pair in range(4):
            at = pair * 128
            context[:, at : at + 128] = pair_attention(
                packed[:, at : at + 128],
                packed[:, width + at : width + at + 128],
                packed[:, 2 * width + at : 2 * width + at + 128],
                same,
            )
        state = state + product(context[...], self_out_ref[...])
        normed = normalize(state, gains_ref[1:2, :]).astype(jnp.bfloat16)
        packed[:, 0:width] = product(normed, query_ref[...]).astype(jnp.bfloat16)
        for pair in range(4):
            at = pair * 128
            context[:, at : at + 128] = pair_attention(
                packed[:, at : at + 128],
                memory[:, at : at + 128],
                memory[:, width + at : width + at + 128],
                held,
            )
        state = state + product(context[...], cross_out_ref[...])
        normed = normalize(state, gains_ref[2:3, :]).astype(jnp.bfloat16)
        hidden = gelu(product(normed, up_ref[...])).astype(jnp.bfloat16)
        state = state + product(hidden, down_ref[...])
        predicted = precise(state, out_ref[...])
        now = jnp.full((8, 128), levels_ref[step].astype(jnp.float32))
        following = levels_ref[jnp.minimum(step + 1, STEPS - 1)]
        after = plan(jnp.full((8, 128), following.astype(jnp.float32)))
        last = jnp.full((8, 128), step) == STEPS - 1
        after = jnp.where(last, 1.0, after)[0:1, 0:10]
        current = plan(now)[0:1, 0:10]
        clean = (sample - jnp.sqrt(1.0 - current) * predicted) / jnp.sqrt(current)
        actions_ref[...] = jnp.sqrt(after) * clean + jnp.sqrt(1.0 - after) * predicted
        return carry

    lax.fori_loop(0, STEPS, one_step, 0)


def denoise(levels, noise, condition, *params):
    whole = pl.BlockSpec(memory_space=VMEM)
    return pl.pallas_call(
        denoise_kernel,
        out_shape=jax.ShapeDtypeStruct((128, 10), jnp.float32),
        in_specs=[pl.BlockSpec(memory_space=pltpu.SMEM)] + [whole] * (2 + len(params)),
        out_specs=whole,
        scratch_shapes=[
            VMEM((8 * KEYS, 1024), jnp.bfloat16),
            VMEM((8, 512), jnp.float32),
            VMEM((128, 1536), jnp.bfloat16),
            VMEM((128, 512), jnp.bfloat16),
        ],
        compiler_params=pltpu.CompilerParams(vmem_limit_bytes=60 * 1024 * 1024),
    )(levels, noise, condition, *params)


def on_device(
    pixels,
    patch_weight,
    position,
    encoder_gains,
    qkv_weight,
    out_weight,
    up_weight,
    down_weight,
    cond_weight,
    time_weight,
    action_in,
    action_pos,
    denoise_gains,
    self_qkv,
    self_out,
    cross_query,
    cross_kv,
    cross_out,
    mix_up,
    mix_down,
    action_out,
    noise,
    timesteps,
):
    local_views, group_count, block_count, patches, pixel_width = pixels.shape
    count = local_views * group_count * block_count
    width = position.shape[1]
    head_size = width // HEADS
    flat = pixels.reshape(count * patches, pixel_width)
    patch_full, qkv_full, out_full, up_full, down_full = (
        lax.all_gather(patch_weight, "mp", axis=0, tiled=True),
        *in_one_piece((qkv_weight, out_weight, up_weight), "mp", 0, 1),
        lax.all_gather(down_weight, "mp", axis=0, tiled=True),
    )
    embedded = product(flat, patch_full)
    state = embedded.reshape(count, patches, width) + position.astype(jnp.float32)
    normed = normalize(state, encoder_gains[0]).astype(jnp.bfloat16).reshape(-1, width)
    packed = (
        product(normed, qkv_full).astype(jnp.bfloat16).reshape(count, patches, 3, HEADS, head_size)
    )
    scores = contract("nqhd,nkhd->nhqk", packed[:, :, 0], packed[:, :, 1]) / math.sqrt(head_size)
    probs = jax.nn.softmax(scores, -1).astype(jnp.bfloat16)
    context = contract("nhqk,nkhd->nqhd", probs, packed[:, :, 2]).astype(jnp.bfloat16)
    state = state + product(context.reshape(-1, width), out_full).reshape(state.shape)
    normed = normalize(state, encoder_gains[1]).astype(jnp.bfloat16).reshape(-1, width)
    hidden = jax.nn.gelu(product(normed, up_full), approximate=False).astype(jnp.bfloat16)
    state = state + product(hidden, down_full).reshape(state.shape)
    side = GRID // 2
    final = normalize(state, encoder_gains[2]).reshape(count, side, 2, side, 2, width)
    cells = side * side
    pooled = jnp.mean(final, axis=(2, 4)).reshape(count, cells, width).astype(jnp.bfloat16)
    condition = product(pooled.reshape(-1, width), cond_weight).astype(jnp.bfloat16)
    condition = jnp.pad(condition.reshape(count, cells, -1), ((0, 0), (0, KEYS - cells), (0, 0)))
    moved = lax.all_to_all(condition, "batch", split_axis=0, concat_axis=0, tiled=True)
    actions = denoise(
        timesteps,
        noise.reshape(-1, noise.shape[-1]),
        moved.reshape(count * KEYS, -1),
        time_weight,
        action_in,
        action_pos,
        denoise_gains,
        self_qkv,
        self_out,
        cross_query,
        cross_kv,
        cross_out,
        mix_up,
        mix_down,
        action_out,
    )
    return actions.reshape(noise.shape)


def solution(mesh):
    return jax.shard_map(
        on_device,
        mesh=mesh,
        in_specs=(
            P("batch", "mp", None, None, None),
            P("mp", None),
            P(),
            P(),
            P("mp", None),
            P("mp", None),
            P("mp", None),
            P("mp", None),
            P(),
            P(),
            P(),
            P(),
            P(),
            P(),
            P(),
            P(),
            P(),
            P(),
            P(),
            P(),
            P(),
            P("mp", "batch", None, None, None),
            P(),
        ),
        out_specs=P("mp", "batch", None, None, None),
        check_vma=False,
    )
```

profile of v0, /device:TPU:0, one launch (start us, length us, event | category | flops | bytes accessed | tf_op | source)
XLA Modules:
  0.0 342.3 jit_solution(17501089927135830361)
XLA Ops:
  7.3 2.3 pad_maximum_fusion
  12.8 45.6 %all-gather.4.cloned.1.call-done = bf16[768,1024]{1,0:T(8,128)(2,1)} async-done(((bf16[48,1024]{1,0:T(8,128)(2,1)}), bf16[768,1024]{1,0:T(8,128)(2,1)}) %all-gather.4.cloned.1.call-update) | async-done | bytes 1572880 | tf_op jit(solution)/shard_map/all_gather | solution.py:215
  58.4 3.4 add_reduce_fusion
  64.1 1.5 reshape.85
  65.6 102.9 %all-gather.6.cloned.1.call-done = bf16[1024,8192]{1,0:T(8,128)(2,1)} async-done(((bf16[64,8192]{1,0:T(8,128)(2,1)}), bf16[1024,8192]{1,0:T(8,128)(2,1)}) %all-gather.6.cloned.1.call-update) | async-done | bytes 16777232 | tf_op jit(solution)/shard_map/all_gather | solution.py:24
  168.5 9.3 %fusion.22 = bf16[800,3072]{1,0:T(8,128)(2,1)} fusion(bf16[800,1024]{1,0:T(8,128)(2,1)} %reshape.85, bf16[1024,8192]{1,0:T(8,128)(2,1)} %all-gather.6.cloned.1.call-done), kind=kOutput, calls=%fused_computation.29 | convolution fusion | flops 5035622400 | bytes 12845056 | tf_op jit(solution)/shard_map/dot_general | solution.py:42
  177.8 13.1 %reshape.95 = bf16[8,100,3,16,64]{4,3,2,1,0:T(8,128)(2,1)} reshape(bf16[800,3072]{1,0:T(8,128)(2,1)} %fusion.22) | data formatting | bytes 9830400 | tf_op jit(solution)/shard_map/reshape | solution.py:223
  190.9 7.1 %fusion.72 = (bf16[8,100,1,16,64]{4,3,2,1,0:T(8,128)(2,1)}, bf16[8,100,1,16,64]{4,3,2,1,0:T(8,128)(2,1)}, bf16[8,100,1,16,64]{4,3,2,1,0:T(8,128)(2,1)}) fusion(bf16[8,100,3,16,64]{4,3,2,1,0:T(8,128)(2,1)} %reshape.95), kind=kLoop, calls=%fused_computation.91 | loop fusion | bytes 9830400 | tf_op jit(solution)/shard_map/slice | solution.py:227
  197.9 4.5 %copy.61 = bf16[8,100,1,16,64]{1,4,3,0,2:T(8,128)(2,1)S(1)} copy(bf16[8,100,1,16,64]{4,3,2,1,0:T(8,128)(2,1)} %get-tuple-element.8) | data formatting | bytes 3276800
  202.4 5.4 %copy.62 = bf16[8,100,1,16,64]{1,4,3,0,2:T(8,128)(2,1)} copy(bf16[8,100,1,16,64]{4,3,2,1,0:T(8,128)(2,1)} %get-tuple-element.9) | data formatting | bytes 3276800
  207.8 5.4 %copy.60 = bf16[8,100,1,16,64]{1,4,3,0,2:T(8,128)(2,1)} copy(bf16[8,100,1,16,64]{4,3,2,1,0:T(8,128)(2,1)} %get-tuple-element.7) | data formatting | bytes 3276800
  213.2 3.6 %fusion.30 = f32[8,16,100,100]{2,3,1,0:T(8,128)S(1)} fusion(bf16[8,100,1,16,64]{1,4,3,0,2:T(8,128)(2,1)} %copy.62, bf16[8,100,1,16,64]{1,4,3,0,2:T(8,128)(2,1)S(1)} %copy.61), kind=kOutput, calls=%fused_computation.42 | convolution fusion | flops 163840000 | bytes 8396800 | tf_op jit(solution)/shard_map/nqhd,nkhd->nhqk/dot_general | solution.py:50
  216.8 7.4 %fusion.74 = (f32[8,16,100]{2,1,0:T(8,128)S(1)}, f32[8,16,100,100]{2,3,1,0:T(8,128)S(1)}) fusion(f32[8,16,100,100]{2,3,1,0:T(8,128)S(1)} %fusion.30), kind=kOutput, calls=%fused_computation.93 | output fusion | flops 5120099 | bytes 10291200 | tf_op jit(solution)/shard_map/sub | solution.py:226
  226.3 4.2 %fusion.75 = (f32[8,100]{1,0:T(8,128)S(1)}, f32[8,100,1024]{2,1,0:T(8,128)S(1)}) fusion(bf16[8,100,1024]{1,2,0:T(8,128)(2,1)S(1)} %bitcast.46, bf16[1024,8192]{1,0:T(8,128)(2,1)} %all-gather.6.cloned.1.call-done, f32[8,100,1024]{2,1,0:T(8,128)S(1)} %copy-done.3, f32[100,1024]{1,0:T(8,128)S(1)} %copy-done.5), kind=kOutput, calls=%fused_computation.94 | convolution fusion | flops 1680178432 | bytes 10701952 | tf_op jit(solution)/shard_map/dot_general | solution.py:42
  234.1 37.6 %fusion.91 = bf16[800,4096]{1,0:T(8,128)(2,1)} fusion(bf16[800,1024]{1,0:T(8,128)(2,1)} %reshape.87, bf16[1024,8192]{1,0:T(8,128)(2,1)} %all-gather.6.cloned.1.call-done), kind=kOutput, calls=%fused_computation.4.clone.clone.1 | convolution fusion | flops 6923878400 | bytes 16580608 | tf_op jit(solution)/shard_map/dot_general | solution.py:42
  271.7 12.5 %fusion.13 = f32[800,1024]{1,0:T(8,128)} fusion(bf16[4096,1024]{1,0:T(8,128)(2,1)} %all-gather.8.cloned.1.call-done, bf16[800,4096]{1,0:T(8,128)(2,1)} %fusion.91), kind=kOutput, calls=%fused_computation.24 | convolution fusion | flops 6710886400 | bytes 18219008 | tf_op jit(solution)/shard_map/dot_general | solution.py:42
  284.1 3.3 reshape.88
  287.5 3.4 %fusion.71 = (f32[8,100]{1,0:T(8,128)S(1)}, f32[8,100,1024]{2,1,0:T(8,128)S(1)}) fusion(f32[8,100,1024]{2,1,0:T(8,128)} %copy-done.1, f32[8,100,1024]{2,1,0:T(8,128)} %reshape.88), kind=kLoop, calls=%fused_computation.90 | loop fusion | flops 1637600 | bytes 9833600 | tf_op jit(solution)/shard_map/reduce_sum | solution.py:29
  291.9 3.6 %copy.52 = f32[8,100,1024]{2,0,1:T(8,128)} copy(f32[8,100,1024]{2,1,0:T(8,128)S(1)} %multiply_multiply_fusion.5) | data formatting | bytes 6553600 | tf_op jit(solution)/shard_map/mul | solution.py:32
  295.5 2.3 reduce_sum.79
  299.5 4.7 %all-to-all-start = ((bf16[8,32,512]{2,1,0:T(8,128)(2,1)}), bf16[8,32,512]{2,1,0:T(8,128)(2,1)S(1)}, u32[]{:S(2)}, u32[]{:S(2)}) async-start(bf16[8,32,512]{2,1,0:T(8,128)(2,1)} %pad.4), calls=%async_computation | async-start | bytes 524288 | tf_op jit(solution)/shard_map/all_to_all | solution.py:238
  305.8 6.0 %all-to-all-done = bf16[8,32,512]{2,1,0:T(8,128)(2,1)S(1)} async-done(((bf16[8,32,512]{2,1,0:T(8,128)(2,1)}), bf16[8,32,512]{2,1,0:T(8,128)(2,1)S(1)}, u32[]{:S(2)}, u32[]{:S(2)}) %all-to-all-start) | async-done | bytes 262176 | tf_op jit(solution)/shard_map/all_to_all | solution.py:238
  312.5 21.7 %shard_map.217 = f32[128,10]{1,0:T(8,128)} custom-call(s32[4]{0:T(128)} %levels_ref.1, f32[128,10]{1,0:T(8,128)} %bitcast.48, bf16[256,512]{1,0:T(8,128)(2,1)} %bitcast.47, f32[512,512]{1,0:T(8,128)} %time_ref.1, f32[10,512]{1,0:T(8,128)} %in_ref.1, f32[16,512]{1,0:T(8,128)} %pos_ref.1, f32[3,512]{1,0:T(4,128)} %gains_ref.1, bf16[512,1536]{1,0:T(8,128)(2,1)} %qkv_ref.1, ...), custom_call_target="tpu_custom_call" | custom-call | tf_op jit(solution)/shard_map/pallas_call | solution.py:169
  334.2 1.6 copy.55
  (53 shorter events, 16.8 us)
Async XLA Ops:
  6.5 291.8 %copy-start = (bf16[1024,512]{1,0:T(8,128)(2,1)S(1)}, bf16[1024,512]{1,0:T(8,128)(2,1)}, u32[]{:S(2)}) copy-start(bf16[1024,512]{1,0:T(8,128)(2,1)} %param.31) | copy-start | bytes 3145732
  6.5 51.8 %all-gather.4.cloned.1.call-start = ((), (), s32[]{:S(2)}) async-start(), calls=%async_computation.1 | async-start | bytes 1671168 | tf_op jit(solution)/shard_map/all_gather | solution.py:215
  7.3 161.2 %all-gather.6.cloned.1.call-start = ((), (), s32[]{:S(2)}) async-start(), calls=%async_computation.2 | async-start | bytes 17825792 | tf_op jit(solution)/shard_map/all_gather | solution.py:24
  9.6 262.1 %all-gather.8.cloned.1.call-start = ((), (), s32[]{:S(2)}) async-start(), calls=%async_computation.3 | async-start | bytes 8912896 | tf_op jit(solution)/shard_map/all_gather | solution.py:217
  11.3 51.1 %copy-start.4 = (f32[100,1024]{1,0:T(8,128)}, f32[100,1024]{1,0:T(8,128)S(1)}, u32[]{:S(2)}) copy-start(f32[100,1024]{1,0:T(8,128)S(1)} %convert_element_type.36) | copy-start | bytes 1228804
  61.7 1.7 copy-start.2
  216.7 7.5 %copy-start.6 = (bf16[8,100,1,16,64]{1,4,3,0,2:T(8,128)(2,1)S(1)}, bf16[8,100,1,16,64]{1,4,3,0,2:T(8,128)(2,1)}, u32[]{:S(2)}) copy-start(bf16[8,100,1,16,64]{1,4,3,0,2:T(8,128)(2,1)} %copy.60) | copy-start | bytes 4915204
  224.2 2.0 copy-start.3
  224.2 2.1 copy-start.5
  230.5 1.8 copy-start.1
  287.5 4.0 %copy-start.10 = (f32[1,1024]{1,0:T(1,128)S(1)}, f32[1,1024]{1,0:T(1,128)}, u32[]{:S(2)}) copy-start(f32[1,1024]{1,0:T(1,128)} %get-tuple-element.10) | copy-start | bytes 12292
  295.5 8.7 %copy-start.9 = (f32[512,10]{0,1:T(8,128)S(1)}, f32[512,10]{0,1:T(8,128)}, u32[]{:S(2)}) copy-start(f32[512,10]{0,1:T(8,128)} %param.43) | copy-start | bytes 61444
  295.5 9.5 %copy-start.8 = (f32[1,1,8,16,10]{3,2,4,1,0:T(8,128)S(1)}, f32[1,1,8,16,10]{3,2,4,1,0:T(8,128)}, u32[]{:S(2)}) copy-start(f32[1,1,8,16,10]{3,2,4,1,0:T(8,128)} %param.44) | copy-start | bytes 15364
  299.5 12.3 %all-to-all-start = ((bf16[8,32,512]{2,1,0:T(8,128)(2,1)}), bf16[8,32,512]{2,1,0:T(8,128)(2,1)S(1)}, u32[]{:S(2)}, u32[]{:S(2)}) async-start(bf16[8,32,512]{2,1,0:T(8,128)(2,1)} %pad.4), calls=%async_computation | async-start | bytes 524288 | tf_op jit(solution)/shard_map/all_to_all | solution.py:238
  311.8 0.7 copy-start.7
Sparse Core Ops, SparseCore 0:
  9.8 48.5 all-gather.3
  60.9 107.5 all-gather.5
  171.0 70.3 all-gather.7
where the time goes:
time: 343 us; the launch traced here: 342 us
  waiting for transfers between devices  156 us (45%)
  matrix products  71.9 us (21%)
  local copies, waits for them, and re-layouts  54.9 us (16%)
  Pallas kernels  21.7 us (6%)
  other arithmetic  19.7 us (6%)
  between operations  13.4 us (4%)
  starting transfers between devices  4.75 us (1%)
    all_gather x1, waiting for transfers between devices, in_one_piece(): result = lax.all_gather(both, axis, axis=dim, tiled=True)  103 us
    dot_general x6, matrix products, product(): return jnp.dot(left, right, preferred_element_type=jnp.float32)  67.2 us
    all_gather x1, waiting for transfers between devices, on_device(): lax.all_gather(patch_weight, 'mp', axis=0, tiled=True)  45.6 us
    pallas_call x1, Pallas kernels, denoise(): pl.pallas_call(denoise_kernel, out_shape=jax.ShapeDtypeStruct((128, 10),...  21.7 us
    unnamed x27, local copies, waits for them, and re-layouts  20.8 us
    reshape x1, local copies, waits for them, and re-layouts, on_device(): product(normed, qkv_full).astype(jnp.bfloat16)  13.1 us
    sub x1, other arithmetic, on_device(): probs = jax.nn.softmax(scores, -1).astype(jnp.bfloat16)  7.43 us
    slice x1, local copies, waits for them, and re-layouts, on_device(): packed[:, :, 2]  7.05 us
  transfers between devices with their start and end apart: 4, of which 3 were waited for; matrix products, arithmetic and copies ran while one was open for 33% of the time, Pallas kernels for 0%

commit v1 on v0

--- a/solution.py
+++ b/solution.py
@@ -7,22 +7,13 @@
 from jax.experimental.pallas import tpu as pltpu
 from jax.sharding import PartitionSpec as P
 
-HEADS = 16
 GRID = 10
-DHEADS = 8
 STEPS = 4
 TMAX = 100
 
 
 norm_eps = 1e-06
 offset = 0.008
-
-
-def in_one_piece(arrays, axis, dim, along):
-    widths = [a.shape[along] for a in arrays]
-    both = jnp.concatenate(arrays, axis=along)
-    result = lax.all_gather(both, axis, axis=dim, tiled=True)
-    return tuple(jnp.split(result, [sum(widths[:k]) for k in range(1, len(widths))], axis=along))
 
 
 def normalize(values, gain):
@@ -44,10 +35,6 @@
 
 def precise(left, right):
     return jnp.dot(left, right, precision=lax.Precision.HIGHEST)
-
-
-def contract(form, left, right):
-    return jnp.einsum(form, left, right, preferred_element_type=jnp.float32)
 
 
 VMEM = pltpu.VMEM
@@ -181,6 +168,448 @@
     )(levels, noise, condition, *params)
 
 
+FRAMES = 8
+ROWS = 112
+LINKS = 24
+CHUNKS = 8
+MESH = pl.DeviceIdType.MESH
+
+
+def encode_kernel(
+    pixels_ref,
+    patch_ref,
+    position_ref,
+    gains_ref,
+    qkv_ref,
+    out_ref,
+    up_ref,
+    down_ref,
+    cond_ref,
+    result_ref,
+    patch_full,
+    qkv_full,
+    out_full,
+    up_full,
+    down_full,
+    pixels,
+    place,
+    state,
+    normed,
+    packed,
+    hidden,
+    pooled,
+    leaving,
+    landed,
+    sent,
+    came,
+    kept,
+    slab_sent,
+    slab_came,
+):
+    batch = lax.axis_index("batch")
+    part = lax.axis_index("mp")
+    near, y = batch // 4, batch % 4
+    core = part % 2
+    z = (part // 2) % 4
+    half = part // 8
+    kind = (y + near + half) % 2
+
+    def at_z(by):
+        return {"mp": (half * 4 + (z + by) % 4) * 2 + core, "batch": batch}
+
+    def at_y(by):
+        return {"batch": near * 4 + (y + by) % 4, "mp": part}
+
+    z_up, z_down, y_up, y_down = at_z(1), at_z(3), at_y(1), at_y(3)
+    inner = {"batch": (1 - near) * 4 + y, "mp": part}
+    cross = {"batch": (1 - near) * 4 + y, "mp": ((1 - half) * 4 + z) * 2 + core}
+    partner = {"batch": batch, "mp": part + 1 - 2 * core}
+
+    chunks = (
+        (patch_ref, patch_full, 48, 0, 1024),
+        (qkv_ref, qkv_full, 64, 0, 1536),
+        (qkv_ref, qkv_full, 64, 1536, 1536),
+        (out_ref, out_full, 64, 0, 1024),
+        (up_ref, up_full, 64, 0, 2048),
+        (up_ref, up_full, 64, 2048, 2048),
+        (down_ref, down_full, 256, 0, 512),
+        (down_ref, down_full, 256, 512, 512),
+    )
+
+    def span(chunk, side, which):
+        start, width = chunk[3], chunk[4]
+        if which == "all":
+            return pl.ds(start, width)
+        if which == "half":
+            return pl.ds(pl.multiple_of(start + side * (width // 2), 128), width // 2)
+        first = start + side * (width // 2) + which * (width // 4)
+        return pl.ds(pl.multiple_of(first, 128), width // 4)
+
+    def region(chunk, where, holder, side, which):
+        other, by = where
+        side_half = 1 - half if other else half
+        owner = (side_half * 4 + (z + by) % 4) * 2 + holder
+        base = pl.multiple_of(owner * chunk[2], 16)
+        return chunk[1].at[pl.ds(base, chunk[2]), span(chunk, side, which)]
+
+    own, below, above, far = (0, 0), (0, 3), (0, 1), (0, 2)
+    x_own, x_below, x_above, x_far = (1, 0), (1, 3), (1, 1), (1, 2)
+    outgoing = (
+        (own, "half", z_up),
+        (own, "half", z_down),
+        (own, "half", cross),
+        (below, 0, z_up),
+        (above, 1, z_down),
+        (x_own, "half", z_up),
+        (x_own, "half", z_down),
+        (far, "half", cross),
+        (below, "half", y_up),
+        (x_below, "half", y_up),
+        (x_far, 0, y_up),
+        (above, "half", y_down),
+        (x_above, "half", y_down),
+        (x_far, 1, y_down),
+        (x_own, "half", inner),
+        (far, "half", inner),
+        (own, "all", partner),
+        (below, "all", partner),
+        (above, "all", partner),
+        (x_own, "all", partner),
+        (x_below, "all", partner),
+        (x_above, "all", partner),
+        (far, "all", partner),
+        (x_far, "all", partner),
+    )
+    arriving = (
+        (below, "half"),
+        (above, "half"),
+        (x_own, "half"),
+        (far, 0),
+        (far, 1),
+        (x_below, "half"),
+        (x_above, "half"),
+        (x_far, "half"),
+        (below, "half"),
+        (x_below, "half"),
+        (x_far, 0),
+        (above, "half"),
+        (x_above, "half"),
+        (x_far, 1),
+        (x_own, "half"),
+        (far, "half"),
+        (own, "all"),
+        (below, "all"),
+        (above, "all"),
+        (x_own, "all"),
+        (x_below, "all"),
+        (x_above, "all"),
+        (far, "all"),
+        (x_far, "all"),
+    )
+
+    def copy_out(k, slot):
+        chunk = chunks[k]
+        where, which, peer = outgoing[slot]
+        target = region(chunk, where, core, kind, which)
+        source = chunk[0].at[:, span(chunk, kind, which)] if where == own else target
+        return pltpu.make_async_remote_copy(
+            src_ref=source,
+            dst_ref=target,
+            send_sem=sent.at[k, slot],
+            recv_sem=came.at[k, slot],
+            device_id=peer,
+            device_id_type=MESH,
+        )
+
+    def keep(k):
+        chunk = chunks[k]
+        return pltpu.make_async_copy(
+            chunk[0].at[:, span(chunk, 0, "all")], region(chunk, own, core, 0, "all"), kept.at[k]
+        )
+
+    def send(k, *slots):
+        for slot in slots:
+            copy_out(k, slot).start()
+
+    def await_slots(k, *slots):
+        for slot in slots:
+            where, which = arriving[slot]
+            holder = core if slot < 16 else 1 - core
+            side = kind if slot < 8 else 1 - kind
+            place_here = region(chunks[k], where, holder, side, which)
+            pltpu.make_async_remote_copy(
+                src_ref=place_here,
+                dst_ref=place_here,
+                send_sem=sent.at[k, slot],
+                recv_sem=came.at[k, slot],
+                device_id=partner,
+                device_id_type=MESH,
+            ).wait_recv()
+
+    def s0(k):
+        send(k, 0, 1, 2)
+        keep(k).start()
+        send(k, 16)
+
+    def s1(k):
+        await_slots(k, 0, 1, 2)
+        send(k, 5, 6, 3, 4, 8, 11, 14)
+
+    def s2(k):
+        await_slots(k, 3, 4, 5, 6)
+        send(k, 7, 9, 12, 15)
+
+    def s3(k):
+        await_slots(k, 8, 11, 14)
+        send(k, 17, 18, 19)
+
+    def s4(k):
+        await_slots(k, 7)
+        send(k, 10, 13)
+
+    def s5(k):
+        await_slots(k, 9, 12, 15)
+        send(k, 20, 21, 22)
+
+    def s6(k):
+        await_slots(k, 10, 13)
+        send(k, 23)
+
+    def s7(k):
+        keep(k).wait()
+        await_slots(k, 16, 17, 18, 19, 20, 21, 22, 23)
+
+    barrier = pltpu.get_barrier_semaphore()
+    for peer in (z_up, z_down, cross, partner):
+        pl.semaphore_signal(barrier, inc=1, device_id=peer, device_id_type=MESH)
+    for by in range(1, FRAMES):
+        peer = {"batch": (batch + by) % FRAMES, "mp": part}
+        pl.semaphore_signal(barrier, inc=1, device_id=peer, device_id_type=MESH)
+    pl.semaphore_wait(barrier, 4 + FRAMES - 1)
+
+    def run(count, body, steps):
+        def turn(i, carry):
+            for when, act in steps:
+                pl.when(i == when)(act)
+            body(i)
+            return carry
+
+        lax.fori_loop(0, count, turn, 0)
+
+    def norm_rows(gain):
+        def one(i):
+            rows = pl.ds(pl.multiple_of(i * ROWS, 16), ROWS)
+            normed[rows, :] = normalize(state[rows, :], gains_ref[gain : gain + 1, :]).astype(
+                jnp.bfloat16
+            )
+
+        return one
+
+    def columns(i, width):
+        return pl.ds(pl.multiple_of(i * width, 128), width)
+
+    s0(0)
+    s0(1)
+    for frame in range(FRAMES):
+        pixels[frame * ROWS + 96 : (frame + 1) * ROWS, :] = jnp.zeros((16, 768), jnp.bfloat16)
+        pixels[frame * ROWS : frame * ROWS + 100, :] = pixels_ref[frame]
+    place[96:ROWS, :] = jnp.zeros((16, 1024), jnp.float32)
+    place[0:100, :] = position_ref[...].astype(jnp.float32)
+    s1(0)
+    s0(2)
+    s2(0)
+    s3(0)
+    s1(1)
+    s0(3)
+    s4(0)
+    s5(0)
+    s2(1)
+    s3(1)
+    s6(0)
+    s7(0)
+
+    def embed(i):
+        cols = columns(i, 512)
+        raw = product(pixels[...], patch_full[:, cols]).reshape(FRAMES, ROWS, 512)
+        state[:, cols] = (raw + place[:, cols]).reshape(FRAMES * ROWS, 512)
+
+    run(2, embed, ())
+    s1(2)
+    s0(4)
+    s4(1)
+    s5(1)
+    run(FRAMES, norm_rows(0), ())
+    s2(2)
+    s3(2)
+    s6(1)
+    s7(1)
+
+    def pack(start):
+        def one(i):
+            cols = columns(start + i, 512)
+            packed[:, cols] = product(normed[...], qkv_full[:, cols]).astype(jnp.bfloat16)
+
+        return one
+
+    def rest():
+        s1(3)
+        s0(5)
+        s4(2)
+        s5(2)
+        s6(2)
+        s7(2)
+
+    run(6, pack(0), ((3, rest),))
+
+    key_at = lax.broadcasted_iota(jnp.int32, (2 * ROWS, ROWS), 1)
+
+    def attend(frame):
+        rows = pl.ds(pl.multiple_of(frame * ROWS, 16), ROWS)
+        for pair in range(8):
+            at = pair * 128
+            normed[rows, at : at + 128] = pair_attention(
+                packed[rows, at : at + 128],
+                packed[rows, 1024 + at : 1152 + at],
+                packed[rows, 2048 + at : 2176 + at],
+                key_at < 100,
+            )
+
+    def steps(*acts):
+        def act():
+            for stage, k in acts:
+                stage(k)
+
+        return act
+
+    run(
+        FRAMES,
+        attend,
+        (
+            (0, steps((s2, 3), (s3, 3), (s1, 4), (s0, 6))),
+            (2, steps((s4, 3), (s5, 3), (s2, 4), (s3, 4))),
+            (3, steps((s6, 3), (s1, 5), (s0, 7))),
+            (4, steps((s4, 4), (s5, 4))),
+            (5, steps((s2, 5), (s3, 5), (s6, 4))),
+            (6, steps((s1, 6), (s4, 5), (s5, 5))),
+            (7, steps((s2, 6), (s3, 6), (s6, 5))),
+        ),
+    )
+    s7(3)
+
+    def project(i):
+        cols = columns(i, 512)
+        state[:, cols] += product(normed[...], out_full[:, cols])
+
+    run(2, project, ())
+    s1(7)
+    s4(6)
+    s5(6)
+    run(FRAMES, norm_rows(1), ())
+    s2(7)
+    s3(7)
+    s6(6)
+    s7(4)
+
+    def grow(i):
+        cols = columns(i, 512)
+        hidden[:, cols] = gelu(product(normed[...], up_full[:, cols])).astype(jnp.bfloat16)
+
+    run(8, grow, ((2, steps((s4, 7), (s5, 7))), (3, steps((s6, 7))), (4, steps((s7, 5)))))
+    s7(6)
+
+    def shrink(i):
+        cols = columns(i, 512)
+        state[:, cols] += product(hidden[...], down_full[:, cols])
+
+    run(2, shrink, ((1, steps((s7, 7))),))
+
+    cell = lax.broadcasted_iota(jnp.int32, (KEYS, ROWS), 0)
+    patch = lax.broadcasted_iota(jnp.int32, (KEYS, ROWS), 1)
+    home = patch // GRID // 2 * (GRID // 2) + patch % GRID // 2
+    share = jnp.where((home == cell) & (patch < 100), 0.25, 0.0).astype(jnp.bfloat16)
+
+    def pool(frame):
+        rows = pl.ds(pl.multiple_of(frame * ROWS, 16), ROWS)
+        final = normalize(state[rows, :], gains_ref[2:3, :])
+        high = final.astype(jnp.bfloat16)
+        low = (final - high.astype(jnp.float32)).astype(jnp.bfloat16)
+        mean = product(share, high) + product(share, low)
+        pooled[pl.ds(pl.multiple_of(frame * KEYS, 16), KEYS), :] = mean.astype(jnp.bfloat16)
+
+    run(FRAMES, pool, ())
+    leaving[...] = (
+        product(pooled[...], cond_ref[...]).astype(jnp.bfloat16).reshape(FRAMES, KEYS, 512)
+    )
+
+    def slab(by):
+        to = (batch + by) % FRAMES
+        return pltpu.make_async_remote_copy(
+            src_ref=leaving.at[to],
+            dst_ref=landed.at[batch],
+            send_sem=slab_sent.at[by],
+            recv_sem=slab_came.at[by],
+            device_id={"batch": to, "mp": part},
+            device_id_type=MESH,
+        )
+
+    for by in range(1, FRAMES):
+        slab(by).start()
+    for by in range(1, FRAMES):
+        source = (batch + FRAMES - by) % FRAMES
+        pltpu.make_async_remote_copy(
+            src_ref=landed.at[source],
+            dst_ref=landed.at[source],
+            send_sem=slab_sent.at[by],
+            recv_sem=slab_came.at[by],
+            device_id=partner,
+            device_id_type=MESH,
+        ).wait_recv()
+        result_ref[source] = landed[source]
+    result_ref[batch] = leaving[batch]
+    for by in range(1, FRAMES):
+        slab(by).wait_send()
+    for k in range(CHUNKS):
+        for slot in range(LINKS):
+            copy_out(k, slot).wait_send()
+
+
+def encode(pixels, patch, position, gains, qkv, out, up, down, cond):
+    bf16, f32 = jnp.bfloat16, jnp.float32
+    whole = pl.BlockSpec(memory_space=VMEM)
+    apart = pl.BlockSpec(memory_space=pl.ANY)
+    tall = FRAMES * ROWS
+    return pl.pallas_call(
+        encode_kernel,
+        out_shape=jax.ShapeDtypeStruct((FRAMES, KEYS, 512), bf16),
+        in_specs=[whole, apart, whole, whole, apart, apart, apart, apart, whole],
+        out_specs=whole,
+        scratch_shapes=[
+            VMEM((768, 1024), bf16),
+            VMEM((1024, 3072), bf16),
+            VMEM((1024, 1024), bf16),
+            VMEM((1024, 4096), bf16),
+            VMEM((4096, 1024), bf16),
+            VMEM((tall, 768), bf16),
+            VMEM((ROWS, 1024), f32),
+            VMEM((tall, 1024), f32),
+            VMEM((tall, 1024), bf16),
+            VMEM((tall, 3072), bf16),
+            VMEM((tall, 4096), bf16),
+            VMEM((FRAMES * KEYS, 1024), bf16),
+            VMEM((FRAMES, KEYS, 512), bf16),
+            VMEM((FRAMES, KEYS, 512), bf16),
+            pltpu.SemaphoreType.DMA((CHUNKS, LINKS)),
+            pltpu.SemaphoreType.DMA((CHUNKS, LINKS)),
+            pltpu.SemaphoreType.DMA((CHUNKS,)),
+            pltpu.SemaphoreType.DMA((FRAMES,)),
+            pltpu.SemaphoreType.DMA((FRAMES,)),
+        ],
+        compiler_params=pltpu.CompilerParams(
+            vmem_limit_bytes=67043328, collective_id=0, has_side_effects=True
+        ),
+    )(pixels, patch, position, gains, qkv, out, up, down, cond)
+
+
 def on_device(
     pixels,
     patch_weight,
@@ -206,40 +635,21 @@
     noise,
     timesteps,
 ):
-    local_views, group_count, block_count, patches, pixel_width = pixels.shape
-    count = local_views * group_count * block_count
-    width = position.shape[1]
-    head_size = width // HEADS
-    flat = pixels.reshape(count * patches, pixel_width)
-    patch_full, qkv_full, out_full, up_full, down_full = (
-        lax.all_gather(patch_weight, "mp", axis=0, tiled=True),
-        *in_one_piece((qkv_weight, out_weight, up_weight), "mp", 0, 1),
-        lax.all_gather(down_weight, "mp", axis=0, tiled=True),
-    )
-    embedded = product(flat, patch_full)
-    state = embedded.reshape(count, patches, width) + position.astype(jnp.float32)
-    normed = normalize(state, encoder_gains[0]).astype(jnp.bfloat16).reshape(-1, width)
-    packed = (
-        product(normed, qkv_full).astype(jnp.bfloat16).reshape(count, patches, 3, HEADS, head_size)
-    )
-    scores = contract("nqhd,nkhd->nhqk", packed[:, :, 0], packed[:, :, 1]) / math.sqrt(head_size)
-    probs = jax.nn.softmax(scores, -1).astype(jnp.bfloat16)
-    context = contract("nhqk,nkhd->nqhd", probs, packed[:, :, 2]).astype(jnp.bfloat16)
-    state = state + product(context.reshape(-1, width), out_full).reshape(state.shape)
-    normed = normalize(state, encoder_gains[1]).astype(jnp.bfloat16).reshape(-1, width)
-    hidden = jax.nn.gelu(product(normed, up_full), approximate=False).astype(jnp.bfloat16)
-    state = state + product(hidden, down_full).reshape(state.shape)
-    side = GRID // 2
-    final = normalize(state, encoder_gains[2]).reshape(count, side, 2, side, 2, width)
-    cells = side * side
-    pooled = jnp.mean(final, axis=(2, 4)).reshape(count, cells, width).astype(jnp.bfloat16)
-    condition = product(pooled.reshape(-1, width), cond_weight).astype(jnp.bfloat16)
-    condition = jnp.pad(condition.reshape(count, cells, -1), ((0, 0), (0, KEYS - cells), (0, 0)))
-    moved = lax.all_to_all(condition, "batch", split_axis=0, concat_axis=0, tiled=True)
+    condition = encode(
+        pixels.reshape(pixels.shape[2:]),
+        patch_weight,
+        position,
+        encoder_gains,
+        qkv_weight,
+        out_weight,
+        up_weight,
+        down_weight,
+        cond_weight,
+    )
     actions = denoise(
         timesteps,
         noise.reshape(-1, noise.shape[-1]),
-        moved.reshape(count * KEYS, -1),
+        condition.reshape(FRAMES * KEYS, -1),
         time_weight,
         action_in,
         action_pos,

time: 343 us -> 146 us (0.43)
  waiting for transfers between devices: 156 us -> 0 us
  Pallas kernels: 21.7 us -> 138 us
  matrix products: 71.9 us -> 0 us
  local copies, waits for them, and re-layouts: 54.9 us -> 7.23 us
  other arithmetic: 19.7 us -> 0 us
  between operations: 13.4 us -> 0.01 us
  starting transfers between devices: 4.75 us -> 0 us
    all_gather x3 -> x0, waiting for transfers between devices: 149 us -> none  [the longest x1 103 us: in_one_piece(): result = lax.all_gather(both, axis, axis=dim, tiled=True)]
    pallas_call x0 -> x1, Pallas kernels: none -> 117 us  [encode(): pl.pallas_call(encode_kernel, out_shape=jax.ShapeDtypeStruct((FRAMES, KEY...]
    dot_general x8 -> x0, matrix products: 71.9 us -> none  [the longest x6 67.2 us: product(): return jnp.dot(left, right, preferred_element_type=jnp.float32)]
    reshape x5 -> x0, local copies, waits for them, and re-layouts: 19.4 us -> none  [the longest x1 13.1 us: on_device(): product(normed, qkv_full).astype(jnp.bfloat16)]
    unnamed x27 -> x3, local copies, waits for them, and re-layouts: 20.8 us -> 5.66 us
    slice x2 -> x0, local copies, waits for them, and re-layouts: 8.5 us -> none  [the longest x1 7.05 us: on_device(): packed[:, :, 2]]
    sub x1 -> x0, other arithmetic: 7.43 us -> none  [on_device(): probs = jax.nn.softmax(scores, -1).astype(jnp.bfloat16)]
    reduce_sum x5 -> x0, other arithmetic: 7.4 us -> none  [the longest x1 3.44 us: normalize(): middle = jnp.mean(values, -1, keepdims=True)]
  transfers between devices with their start and end apart: 4 -> 0, of which waited for: 3 -> 0; matrix products, arithmetic and copies ran while one was open for 33% -> 0% of each run, Pallas kernels for 0% -> 0%
where the time goes in v1:
time: 146 us
  Pallas kernels  138 us (95%)
  local copies, waits for them, and re-layouts  7.23 us (5%)
    pallas_call x1, Pallas kernels, encode(): pl.pallas_call(encode_kernel, out_shape=jax.ShapeDtypeStruct((FRAMES, KEY...  117 us
    pallas_call x1, Pallas kernels, denoise(): pl.pallas_call(denoise_kernel, out_shape=jax.ShapeDtypeStruct((128, 10),...  21.7 us
    unnamed x3, local copies, waits for them, and re-layouts  5.66 us

profile of v1, /device:TPU:0, one launch (start us, length us, event | category | flops | bytes accessed | tf_op | source)
XLA Modules:
  0.0 145.6 jit_solution(7994436133855584276)
XLA Ops:
  0.0 2.6 %copy.29 = bf16[1,1,8,100,768]{4,3,2,1,0:T(8,128)(2,1)} copy(bf16[1,1,8,100,768]{4,2,3,1,0:T(8,128)(2,1)} %param.23) | data formatting | bytes 2457600 | tf_op args[0]
  2.6 116.6 %shard_map.217 = bf16[8,32,512]{2,1,0:T(8,128)(2,1)} custom-call(bf16[8,100,768]{2,1,0:T(8,128)(2,1)} %bitcast.6, bf16[48,1024]{1,0:T(8,128)(2,1)} %patch_ref.1, bf16[100,1024]{1,0:T(8,128)(2,1)} %position_ref.1, f32[3,1024]{1,0:T(4,128)} %gains_ref.2, bf16[64,3072]{1,0:T(8,128)(2,1)} %qkv_ref.2, bf16[64,1024]{1,0:T(8,128)(2,1)} %out_ref.2, ...), custom_call_target="tpu_custom_call" | custom-call | tf_op jit(solution)/shard_map/pallas_call | solution.py:581
  119.2 1.6 %copy.26.out_ref = f32[512,10]{1,0:T(8,128)} copy(f32[512,10]{0,1:T(8,128)} %param.43) | data formatting | bytes 40960 | tf_op args[20]
  120.8 1.5 %copy.24 = f32[1,1,8,16,10]{4,3,2,1,0:T(8,128)} copy(f32[1,1,8,16,10]{3,2,4,1,0:T(8,128)} %param.44) | data formatting | bytes 10240 | tf_op args[21]
  122.3 21.7 %shard_map.218 = f32[128,10]{1,0:T(8,128)} custom-call(s32[4]{0:T(128)} %levels_ref.1, f32[128,10]{1,0:T(8,128)} %bitcast.9, bf16[256,512]{1,0:T(8,128)(2,1)} %bitcast.7, f32[512,512]{1,0:T(8,128)} %time_ref.1, f32[10,512]{1,0:T(8,128)} %in_ref.1, f32[16,512]{1,0:T(8,128)} %pos_ref.1, f32[3,512]{1,0:T(4,128)} %gains_ref.3, bf16[512,1536]{1,0:T(8,128)(2,1)} %qkv_ref.3, ...), custom_call_target="tpu_custom_call" | custom-call | tf_op jit(solution)/shard_map/pallas_call | solution.py:156
  144.0 1.6 %copy.27 = f32[1,1,8,16,10]{3,2,4,1,0:T(8,128)} copy(f32[1,1,8,16,10]{4,3,2,1,0:T(8,128)} %bitcast.8) | data formatting | bytes 10240 | tf_op jit(solution)/shard_map/reshape | solution.py:666

commit v2 on v1

--- a/solution.py
+++ b/solution.py
@@ -1,3 +1,4 @@
+import functools
 import math
 
 import jax
@@ -87,6 +88,10 @@
     stamps,
     packed,
     context,
+    flat,
+    sample_now,
+    widened_in,
+    widened_out,
 ):
     width = 512
     rows = 128
@@ -99,7 +104,13 @@
     phase = level * jnp.exp(order * (-math.log(10000.0) / (width // 2)))
     waves = jnp.concatenate([jnp.sin(phase), jnp.cos(phase)], axis=1)
     stamps[...] = precise(waves, time_ref[...])
-    actions_ref[...] = noise_ref[...]
+    for widened, given in ((widened_in, in_ref), (widened_out, out_ref)):
+        widened[8:16, :] = jnp.zeros((8, width), jnp.float32)
+        widened[0:10, :] = given[...]
+    flat[...] = jnp.zeros_like(flat)
+    for cand in range(8):
+        flat[0:10, cand * 16 : cand * 16 + 16] = noise_ref[:, cand, :]
+    sample_now[...] = flat[...].T
 
     own = lax.broadcasted_iota(jnp.int32, (2 * rows, rows), 0)
     other = lax.broadcasted_iota(jnp.int32, (2 * rows, rows), 1)
@@ -108,8 +119,8 @@
     held = lax.rem(slot, KEYS) < 25
 
     def one_step(step, carry):
-        sample = actions_ref[...]
-        state = precise(sample, in_ref[...])
+        sample = sample_now[...]
+        state = precise(sample, widened_in[...])
         state = (state.reshape(8, 16, width) + pos_ref[...]).reshape(rows, width)
         state = state + stamps[pl.ds(step, 1), :]
         normed = normalize(state, gains_ref[0:1, :]).astype(jnp.bfloat16)
@@ -137,25 +148,34 @@
         normed = normalize(state, gains_ref[2:3, :]).astype(jnp.bfloat16)
         hidden = gelu(product(normed, up_ref[...])).astype(jnp.bfloat16)
         state = state + product(hidden, down_ref[...])
-        predicted = precise(state, out_ref[...])
+        predicted = lax.dot_general(
+            state,
+            widened_out[...],
+            (((1,), (1,)), ((), ())),
+            precision=lax.Precision.HIGHEST,
+            preferred_element_type=jnp.float32,
+        )
         now = jnp.full((8, 128), levels_ref[step].astype(jnp.float32))
         following = levels_ref[jnp.minimum(step + 1, STEPS - 1)]
         after = plan(jnp.full((8, 128), following.astype(jnp.float32)))
         last = jnp.full((8, 128), step) == STEPS - 1
-        after = jnp.where(last, 1.0, after)[0:1, 0:10]
-        current = plan(now)[0:1, 0:10]
+        after = jnp.where(last, 1.0, after)[0:1, 0:16]
+        current = plan(now)[0:1, 0:16]
         clean = (sample - jnp.sqrt(1.0 - current) * predicted) / jnp.sqrt(current)
-        actions_ref[...] = jnp.sqrt(after) * clean + jnp.sqrt(1.0 - after) * predicted
+        sample_now[...] = jnp.sqrt(after) * clean + jnp.sqrt(1.0 - after) * predicted
         return carry
 
     lax.fori_loop(0, STEPS, one_step, 0)
+    flat[...] = sample_now[...].T
+    for cand in range(8):
+        actions_ref[:, cand, :] = flat[0:10, cand * 16 : cand * 16 + 16]
 
 
 def denoise(levels, noise, condition, *params):
     whole = pl.BlockSpec(memory_space=VMEM)
     return pl.pallas_call(
         denoise_kernel,
-        out_shape=jax.ShapeDtypeStruct((128, 10), jnp.float32),
+        out_shape=jax.ShapeDtypeStruct((10, 8, 16), jnp.float32),
         in_specs=[pl.BlockSpec(memory_space=pltpu.SMEM)] + [whole] * (2 + len(params)),
         out_specs=whole,
         scratch_shapes=[
@@ -163,6 +183,10 @@
             VMEM((8, 512), jnp.float32),
             VMEM((128, 1536), jnp.bfloat16),
             VMEM((128, 512), jnp.bfloat16),
+            VMEM((16, 128), jnp.float32),
+            VMEM((128, 16), jnp.float32),
+            VMEM((16, 512), jnp.float32),
+            VMEM((16, 512), jnp.float32),
         ],
         compiler_params=pltpu.CompilerParams(vmem_limit_bytes=60 * 1024 * 1024),
     )(levels, noise, condition, *params)
@@ -173,6 +197,57 @@
 LINKS = 24
 CHUNKS = 8
 MESH = pl.DeviceIdType.MESH
+PLAN = {
+    "prepare": (
+        (0, "a0", "a1", "a2", "b0", "o4", "c0", "b1", "c1", "d0", "o2", "b2", "o5", "a3",),
+    ),
+    "embed": (
+        (0, "c2", "e0", "d1", "f1", "g0", "e1", "f0", "o0", "a4", "o1", "d2", "c3", "h0", "i0", "g1", "f2", "a5", "b3", "a6", "a7", "o7", "z0",),
+        (1, "e2", "h1",),
+    ),
+    "first_norm": (
+        (0, "i1",),
+        (1, "o3",),
+        (5, "g2",),
+    ),
+    "qkv": (
+        (0, "z1",),
+        (1, "h2", "c4",),
+        (2, "b4", "i2", "e3",),
+        (3, "d3", "f3", "b5", "c5", "z2",),
+    ),
+    "att": (
+        (0, "f4", "b6",),
+        (2, "h3", "g3", "c6", "b7",),
+        (3, "d4", "f5", "e4",),
+        (4, "d5", "c7",),
+        (6, "g4",),
+        (7, "e5", "i3", "d6",),
+    ),
+    "out": (
+        (0, "o6", "z3", "e6", "h4",),
+        (1, "g5",),
+    ),
+    "second_norm": (
+        (2, "i4",),
+        (3, "d7", "h5", "f6", "e7",),
+        (4, "g6",),
+    ),
+    "up": (
+        (0, "z4",),
+        (2, "i5",),
+        (3, "h6", "g7",),
+        (4, "z5",),
+        (6, "i6",),
+        (7, "h7",),
+    ),
+    "down": (
+        (0, "f7", "i7", "z6",),
+        (1, "z7",),
+    ),
+    "tail": (
+    ),
+}
 
 
 def encode_kernel(
@@ -191,6 +266,7 @@
     out_full,
     up_full,
     down_full,
+    spread,
     pixels,
     place,
     state,
@@ -346,38 +422,30 @@
                 device_id_type=MESH,
             ).wait_recv()
 
-    def s0(k):
-        send(k, 0, 1, 2)
-        keep(k).start()
-        send(k, 16)
-
-    def s1(k):
-        await_slots(k, 0, 1, 2)
-        send(k, 5, 6, 3, 4, 8, 11, 14)
-
-    def s2(k):
-        await_slots(k, 3, 4, 5, 6)
-        send(k, 7, 9, 12, 15)
-
-    def s3(k):
-        await_slots(k, 8, 11, 14)
-        send(k, 17, 18, 19)
-
-    def s4(k):
-        await_slots(k, 7)
-        send(k, 10, 13)
-
-    def s5(k):
-        await_slots(k, 9, 12, 15)
-        send(k, 20, 21, 22)
-
-    def s6(k):
-        await_slots(k, 10, 13)
-        send(k, 23)
-
-    def s7(k):
-        keep(k).wait()
-        await_slots(k, 16, 17, 18, 19, 20, 21, 22, 23)
+    moves = {
+        "a": ((), (0, 1, 2)),
+        "o": ((), (16,)),
+        "b": ((0, 1), (3, 4, 8, 11)),
+        "c": ((2,), (5, 6, 14)),
+        "d": ((3, 4), (7, 15)),
+        "e": ((5, 6), (9, 12)),
+        "f": ((8, 11, 14), (17, 18, 19)),
+        "g": ((7,), (10, 13)),
+        "h": ((9, 12, 15), (20, 21, 22)),
+        "i": ((10, 13), (23,)),
+        "z": ((16, 17, 18, 19, 20, 21, 22, 23), ()),
+    }
+
+    def move(names):
+        for name in names:
+            k = int(name[1])
+            awaited, sending = moves[name[0]]
+            if name[0] == "o":
+                keep(k).start()
+            if name[0] == "z":
+                keep(k).wait()
+            await_slots(k, *awaited)
+            send(k, *sending)
 
     barrier = pltpu.get_barrier_semaphore()
     for peer in (z_up, z_down, cross, partner):
@@ -387,10 +455,10 @@
         pl.semaphore_signal(barrier, inc=1, device_id=peer, device_id_type=MESH)
     pl.semaphore_wait(barrier, 4 + FRAMES - 1)
 
-    def run(count, body, steps):
+    def run(count, body, stage):
         def turn(i, carry):
-            for when, act in steps:
-                pl.when(i == when)(act)
+            for when, *names in PLAN.get(stage, ()):
+                pl.when(i == when)(functools.partial(move, names))
             body(i)
             return carry
 
@@ -408,58 +476,32 @@
     def columns(i, width):
         return pl.ds(pl.multiple_of(i * width, 128), width)
 
-    s0(0)
-    s0(1)
+    move(PLAN["prepare"][0][1:])
+    for part_at in range(6):
+        lanes = pl.ds(part_at * 128, 128)
+        spread[part_at] = pixels_ref[:, :, lanes].astype(jnp.float32).reshape(800, 128)
     for frame in range(FRAMES):
         pixels[frame * ROWS + 96 : (frame + 1) * ROWS, :] = jnp.zeros((16, 768), jnp.bfloat16)
-        pixels[frame * ROWS : frame * ROWS + 100, :] = pixels_ref[frame]
+        for part_at in range(6):
+            pixels[frame * ROWS : frame * ROWS + 100, part_at * 128 : part_at * 128 + 128] = spread[
+                part_at, pl.ds(frame, 100, stride=FRAMES), :
+            ].astype(jnp.bfloat16)
     place[96:ROWS, :] = jnp.zeros((16, 1024), jnp.float32)
     place[0:100, :] = position_ref[...].astype(jnp.float32)
-    s1(0)
-    s0(2)
-    s2(0)
-    s3(0)
-    s1(1)
-    s0(3)
-    s4(0)
-    s5(0)
-    s2(1)
-    s3(1)
-    s6(0)
-    s7(0)
 
     def embed(i):
         cols = columns(i, 512)
         raw = product(pixels[...], patch_full[:, cols]).reshape(FRAMES, ROWS, 512)
         state[:, cols] = (raw + place[:, cols]).reshape(FRAMES * ROWS, 512)
 
-    run(2, embed, ())
-    s1(2)
-    s0(4)
-    s4(1)
-    s5(1)
-    run(FRAMES, norm_rows(0), ())
-    s2(2)
-    s3(2)
-    s6(1)
-    s7(1)
-
-    def pack(start):
-        def one(i):
-            cols = columns(start + i, 512)
-            packed[:, cols] = product(normed[...], qkv_full[:, cols]).astype(jnp.bfloat16)
-
-        return one
-
-    def rest():
-        s1(3)
-        s0(5)
-        s4(2)
-        s5(2)
-        s6(2)
-        s7(2)
-
-    run(6, pack(0), ((3, rest),))
+    run(2, embed, "embed")
+    run(FRAMES, norm_rows(0), "first_norm")
+
+    def pack(i):
+        cols = columns(i, 512)
+        packed[:, cols] = product(normed[...], qkv_full[:, cols]).astype(jnp.bfloat16)
+
+    run(6, pack, "qkv")
 
     key_at = lax.broadcasted_iota(jnp.int32, (2 * ROWS, ROWS), 1)
 
@@ -474,54 +516,26 @@
                 key_at < 100,
             )
 
-    def steps(*acts):
-        def act():
-            for stage, k in acts:
-                stage(k)
-
-        return act
-
-    run(
-        FRAMES,
-        attend,
-        (
-            (0, steps((s2, 3), (s3, 3), (s1, 4), (s0, 6))),
-            (2, steps((s4, 3), (s5, 3), (s2, 4), (s3, 4))),
-            (3, steps((s6, 3), (s1, 5), (s0, 7))),
-            (4, steps((s4, 4), (s5, 4))),
-            (5, steps((s2, 5), (s3, 5), (s6, 4))),
-            (6, steps((s1, 6), (s4, 5), (s5, 5))),
-            (7, steps((s2, 6), (s3, 6), (s6, 5))),
-        ),
-    )
-    s7(3)
+    run(FRAMES, attend, "att")
 
     def project(i):
         cols = columns(i, 512)
         state[:, cols] += product(normed[...], out_full[:, cols])
 
-    run(2, project, ())
-    s1(7)
-    s4(6)
-    s5(6)
-    run(FRAMES, norm_rows(1), ())
-    s2(7)
-    s3(7)
-    s6(6)
-    s7(4)
+    run(2, project, "out")
+    run(FRAMES, norm_rows(1), "second_norm")
 
     def grow(i):
         cols = columns(i, 512)
         hidden[:, cols] = gelu(product(normed[...], up_full[:, cols])).astype(jnp.bfloat16)
 
-    run(8, grow, ((2, steps((s4, 7), (s5, 7))), (3, steps((s6, 7))), (4, steps((s7, 5)))))
-    s7(6)
+    run(8, grow, "up")
 
     def shrink(i):
         cols = columns(i, 512)
         state[:, cols] += product(hidden[...], down_full[:, cols])
 
-    run(2, shrink, ((1, steps((s7, 7))),))
+    run(2, shrink, "down")
 
     cell = lax.broadcasted_iota(jnp.int32, (KEYS, ROWS), 0)
     patch = lax.broadcasted_iota(jnp.int32, (KEYS, ROWS), 1)
@@ -536,7 +550,7 @@
         mean = product(share, high) + product(share, low)
         pooled[pl.ds(pl.multiple_of(frame * KEYS, 16), KEYS), :] = mean.astype(jnp.bfloat16)
 
-    run(FRAMES, pool, ())
+    run(FRAMES, pool, "tail")
     leaving[...] = (
         product(pooled[...], cond_ref[...]).astype(jnp.bfloat16).reshape(FRAMES, KEYS, 512)
     )
@@ -589,6 +603,7 @@
             VMEM((1024, 1024), bf16),
             VMEM((1024, 4096), bf16),
             VMEM((4096, 1024), bf16),
+            VMEM((6, 800, 128), f32),
             VMEM((tall, 768), bf16),
             VMEM((ROWS, 1024), f32),
             VMEM((tall, 1024), f32),
@@ -636,7 +651,7 @@
     timesteps,
 ):
     condition = encode(
-        pixels.reshape(pixels.shape[2:]),
+        jnp.transpose(pixels.reshape(pixels.shape[2:]), (1, 0, 2)),
         patch_weight,
         position,
         encoder_gains,
@@ -648,7 +663,7 @@
     )
     actions = denoise(
         timesteps,
-        noise.reshape(-1, noise.shape[-1]),
+        jnp.transpose(noise.reshape(noise.shape[2:]), (2, 0, 1)),
         condition.reshape(FRAMES * KEYS, -1),
         time_weight,
         action_in,
@@ -661,9 +676,9 @@
         cross_out,
         mix_up,
         mix_down,
-        action_out,
+        action_out.T,
     )
-    return actions.reshape(noise.shape)
+    return jnp.transpose(actions, (1, 2, 0)).reshape(noise.shape)
 
 
 def solution(mesh):

time: 146 us -> 116 us (0.79)
  Pallas kernels: 138 us -> 116 us
  local copies, waits for them, and re-layouts: 7.23 us -> 0 us
    pallas_call x1, Pallas kernels: 117 us -> 90.6 us  [encode(): pl.pallas_call(encode_kernel, out_shape=jax.ShapeDtypeStruct((FRAMES, KEY...]
    unnamed x3 -> x0, local copies, waits for them, and re-layouts: 5.66 us -> none
    pallas_call x1, Pallas kernels: 21.7 us -> 25 us  [denoise(): pl.pallas_call(denoise_kernel, out_shape=jax.ShapeDtypeStruct((10, 8, 16)...]
    reshape x1 -> x0, local copies, waits for them, and re-layouts: 1.57 us -> none  [on_device(): return actions.reshape(noise.shape)]
where the time goes in v2:
time: 116 us
  Pallas kernels  116 us (100%)
    pallas_call x1, Pallas kernels, encode(): pl.pallas_call(encode_kernel, out_shape=jax.ShapeDtypeStruct((FRAMES, KEY...  90.6 us
    pallas_call x1, Pallas kernels, denoise(): pl.pallas_call(denoise_kernel, out_shape=jax.ShapeDtypeStruct((10, 8, 16)...  25 us

profile of v2, /device:TPU:0, one launch (start us, length us, event | category | flops | bytes accessed | tf_op | source)
XLA Modules:
  0.0 115.6 jit_solution(470198880166855065)
XLA Ops:
  0.0 90.6 %shard_map.217 = bf16[8,32,512]{2,1,0:T(8,128)(2,1)} custom-call(bf16[100,8,768]{2,1,0:T(8,128)(2,1)} %bitcast.11, bf16[48,1024]{1,0:T(8,128)(2,1)} %patch_ref.1, bf16[100,1024]{1,0:T(8,128)(2,1)} %position_ref.1, f32[3,1024]{1,0:T(4,128)} %gains_ref.2, bf16[64,3072]{1,0:T(8,128)(2,1)} %qkv_ref.2, bf16[64,1024]{1,0:T(8,128)(2,1)} %out_ref.1, ...), custom_call_target="tpu_custom_call" | custom-call | tf_op jit(solution)/shard_map/pallas_call | solution.py:595
  90.6 25.0 %shard_map.218 = f32[10,8,16]{2,1,0:T(8,128)} custom-call(s32[4]{0:T(128)} %levels_ref.1, f32[10,8,16]{2,1,0:T(8,128)} %bitcast.13, bf16[256,512]{1,0:T(8,128)(2,1)} %bitcast.12, f32[512,512]{1,0:T(8,128)} %time_ref.1, f32[10,512]{1,0:T(8,128)} %in_ref.1, f32[16,512]{1,0:T(8,128)} %pos_ref.1, f32[3,512]{1,0:T(4,128)} %gains_ref.3, ...), custom_call_target="tpu_custom_call" | custom-call | tf_op jit(solution)/shard_map/pallas_call | solution.py:176

commit v3 on v2

--- a/solution.py
+++ b/solution.py
@@ -54,10 +54,11 @@
     scores = lax.dot_general(
         stacked_heads(query), keys, (((1,), (1,)), ((), ())), preferred_element_type=jnp.float32
     )
-    scores = jnp.where(allowed, scores * 0.125, -1e30)
+    scores = jnp.where(allowed, scores * (0.125 * math.log2(math.e)), -1e30)
     top = jnp.max(scores, axis=-1, keepdims=True)
-    grown = jnp.exp(scores - top)
-    probs = (grown / jnp.sum(grown, axis=-1, keepdims=True)).astype(jnp.bfloat16)
+    grown = jnp.exp2(scores - top)
+    inverse = 1.0 / jnp.sum(grown, axis=-1, keepdims=True)
+    probs = (grown * inverse).astype(jnp.bfloat16)
     both = jnp.dot(probs, values, preferred_element_type=jnp.float32)
     lane = lax.broadcasted_iota(jnp.int32, (rows, 128), 1)
     return jnp.where(lane < 64, both[:rows], both[rows:]).astype(jnp.bfloat16)
@@ -67,10 +68,10 @@
     return 0.5 * values * (1.0 + lax.erf(values * math.sqrt(0.5)))
 
 
-def denoise_kernel(
+def denoiser(
     levels_ref,
+    condition,
     noise_ref,
-    condition_ref,
     time_ref,
     in_ref,
     pos_ref,
@@ -92,35 +93,17 @@
     sample_now,
     widened_in,
     widened_out,
+    out_columns,
+    held_state,
 ):
     width = 512
     rows = 128
-    memory[...] = product(condition_ref[...], kv_ref[...]).astype(jnp.bfloat16)
-    row = lax.broadcasted_iota(jnp.int32, (8, width // 2), 0)
-    level = jnp.zeros((8, width // 2), jnp.float32)
-    for step in range(STEPS):
-        level = jnp.where(row == step, levels_ref[step].astype(jnp.float32), level)
-    order = lax.broadcasted_iota(jnp.int32, (8, width // 2), 1).astype(jnp.float32)
-    phase = level * jnp.exp(order * (-math.log(10000.0) / (width // 2)))
-    waves = jnp.concatenate([jnp.sin(phase), jnp.cos(phase)], axis=1)
-    stamps[...] = precise(waves, time_ref[...])
-    for widened, given in ((widened_in, in_ref), (widened_out, out_ref)):
-        widened[8:16, :] = jnp.zeros((8, width), jnp.float32)
-        widened[0:10, :] = given[...]
-    flat[...] = jnp.zeros_like(flat)
-    for cand in range(8):
-        flat[0:10, cand * 16 : cand * 16 + 16] = noise_ref[:, cand, :]
-    sample_now[...] = flat[...].T
-
-    own = lax.broadcasted_iota(jnp.int32, (2 * rows, rows), 0)
-    other = lax.broadcasted_iota(jnp.int32, (2 * rows, rows), 1)
-    same = lax.rem(own, rows) // 16 == other // 16
-    slot = lax.broadcasted_iota(jnp.int32, (2 * rows, 8 * KEYS), 1)
-    held = lax.rem(slot, KEYS) < 25
-
-    def one_step(step, carry):
-        sample = sample_now[...]
-        state = precise(sample, widened_in[...])
+
+    def first_half(step):
+        own = lax.broadcasted_iota(jnp.int32, (2 * rows, rows), 0)
+        other = lax.broadcasted_iota(jnp.int32, (2 * rows, rows), 1)
+        same = lax.rem(own, rows) // 16 == other // 16
+        state = precise(sample_now[...], widened_in[...])
         state = (state.reshape(8, 16, width) + pos_ref[...]).reshape(rows, width)
         state = state + stamps[pl.ds(step, 1), :]
         normed = normalize(state, gains_ref[0:1, :]).astype(jnp.bfloat16)
@@ -133,7 +116,32 @@
                 packed[:, 2 * width + at : 2 * width + at + 128],
                 same,
             )
-        state = state + product(context[...], self_out_ref[...])
+        held_state[...] = state + product(context[...], self_out_ref[...])
+
+    def begin():
+        row = lax.broadcasted_iota(jnp.int32, (8, width // 2), 0)
+        level = jnp.zeros((8, width // 2), jnp.float32)
+        for step in range(STEPS):
+            level = jnp.where(row == step, levels_ref[step].astype(jnp.float32), level)
+        order = lax.broadcasted_iota(jnp.int32, (8, width // 2), 1).astype(jnp.float32)
+        phase = level * jnp.exp(order * (-math.log(10000.0) / (width // 2)))
+        waves = jnp.concatenate([jnp.sin(phase), jnp.cos(phase)], axis=1)
+        stamps[...] = precise(waves, time_ref[...])
+        for widened, given in ((widened_in, in_ref), (widened_out, out_ref)):
+            widened[8:16, :] = jnp.zeros((8, width), jnp.float32)
+            widened[0:10, :] = given[...]
+        out_columns[...] = widened_out[...].T
+        flat[...] = jnp.zeros_like(flat)
+        for cand in range(8):
+            flat[0:10, cand * 16 : cand * 16 + 16] = noise_ref[:, cand, :]
+        sample_now[...] = flat[...].T
+        first_half(0)
+
+    def one_step(step, carry):
+        slot = lax.broadcasted_iota(jnp.int32, (2 * rows, 8 * KEYS), 1)
+        held = lax.rem(slot, KEYS) < 25
+        sample = sample_now[...]
+        state = held_state[...]
         normed = normalize(state, gains_ref[1:2, :]).astype(jnp.bfloat16)
         packed[:, 0:width] = product(normed, query_ref[...]).astype(jnp.bfloat16)
         for pair in range(4):
@@ -148,13 +156,7 @@
         normed = normalize(state, gains_ref[2:3, :]).astype(jnp.bfloat16)
         hidden = gelu(product(normed, up_ref[...])).astype(jnp.bfloat16)
         state = state + product(hidden, down_ref[...])
-        predicted = lax.dot_general(
-            state,
-            widened_out[...],
-            (((1,), (1,)), ((), ())),
-            precision=lax.Precision.HIGHEST,
-            preferred_element_type=jnp.float32,
-        )
+        predicted = precise(state, out_columns[...])
         now = jnp.full((8, 128), levels_ref[step].astype(jnp.float32))
         following = levels_ref[jnp.minimum(step + 1, STEPS - 1)]
         after = plan(jnp.full((8, 128), following.astype(jnp.float32)))
@@ -163,33 +165,19 @@
         current = plan(now)[0:1, 0:16]
         clean = (sample - jnp.sqrt(1.0 - current) * predicted) / jnp.sqrt(current)
         sample_now[...] = jnp.sqrt(after) * clean + jnp.sqrt(1.0 - after) * predicted
+        pl.when(step < STEPS - 1)(lambda: first_half(step + 1))
         return carry
 
-    lax.fori_loop(0, STEPS, one_step, 0)
-    flat[...] = sample_now[...].T
-    for cand in range(8):
-        actions_ref[:, cand, :] = flat[0:10, cand * 16 : cand * 16 + 16]
-
-
-def denoise(levels, noise, condition, *params):
-    whole = pl.BlockSpec(memory_space=VMEM)
-    return pl.pallas_call(
-        denoise_kernel,
-        out_shape=jax.ShapeDtypeStruct((10, 8, 16), jnp.float32),
-        in_specs=[pl.BlockSpec(memory_space=pltpu.SMEM)] + [whole] * (2 + len(params)),
-        out_specs=whole,
-        scratch_shapes=[
-            VMEM((8 * KEYS, 1024), jnp.bfloat16),
-            VMEM((8, 512), jnp.float32),
-            VMEM((128, 1536), jnp.bfloat16),
-            VMEM((128, 512), jnp.bfloat16),
-            VMEM((16, 128), jnp.float32),
-            VMEM((128, 16), jnp.float32),
-            VMEM((16, 512), jnp.float32),
-            VMEM((16, 512), jnp.float32),
-        ],
-        compiler_params=pltpu.CompilerParams(vmem_limit_bytes=60 * 1024 * 1024),
-    )(levels, noise, condition, *params)
+    def finish():
+        memory[...] = product(condition[...].reshape(8 * KEYS, width), kv_ref[...]).astype(
+            jnp.bfloat16
+        )
+        lax.fori_loop(0, STEPS, one_step, 0)
+        flat[...] = sample_now[...].T
+        for cand in range(8):
+            actions_ref[:, cand, :] = flat[0:10, cand * 16 : cand * 16 + 16]
+
+    return begin, finish
 
 
 FRAMES = 8
@@ -199,50 +187,47 @@
 MESH = pl.DeviceIdType.MESH
 PLAN = {
     "prepare": (
-        (0, "a0", "a1", "a2", "b0", "o4", "c0", "b1", "c1", "d0", "o2", "b2", "o5", "a3",),
+        ("a0", "a1", "o0", "a2", "o1",),
+        ("b0", "c0", "b1", "c1", "o5", "a3", "o7", "d0", "b2", "e0", "c2", "d1", "g0", "a4", "f0", "f1", "o2", "o3", "c3", "e1",),
+        ("h0", "g1", "d2", "i0", "e2", "a5", "b3", "f2", "h1", "z0",),
     ),
     "embed": (
-        (0, "c2", "e0", "d1", "f1", "g0", "e1", "f0", "o0", "a4", "o1", "d2", "c3", "h0", "i0", "g1", "f2", "a5", "b3", "a6", "a7", "o7", "z0",),
-        (1, "e2", "h1",),
     ),
     "first_norm": (
         (0, "i1",),
-        (1, "o3",),
-        (5, "g2",),
+        (2, "c4",),
+        (3, "g2",),
+        (6, "b4",),
+        (7, "z1", "h2",),
     ),
     "qkv": (
-        (0, "z1",),
-        (1, "h2", "c4",),
-        (2, "b4", "i2", "e3",),
-        (3, "d3", "f3", "b5", "c5", "z2",),
+        (0, "a6", "o4",),
+        (2, "i2", "f3", "e3", "d3", "b5",),
+        (3, "c5", "z2",),
+        (4, "e4",),
+        (5, "d4", "a7", "f4",),
     ),
     "att": (
-        (0, "f4", "b6",),
-        (2, "h3", "g3", "c6", "b7",),
-        (3, "d4", "f5", "e4",),
-        (4, "d5", "c7",),
-        (6, "g4",),
-        (7, "e5", "i3", "d6",),
+        (0, "g3",),
+        (2, "h3", "d5",),
+        (3, "b6",),
+        (4, "i3", "g4", "f5", "h4", "c6",),
+        (5, "e5",),
+        (7, "d6", "b7", "z3", "c7", "i4", "g5",),
     ),
     "out": (
-        (0, "o6", "z3", "e6", "h4",),
-        (1, "g5",),
     ),
     "second_norm": (
-        (2, "i4",),
-        (3, "d7", "h5", "f6", "e7",),
-        (4, "g6",),
+        (1, "d7", "e6", "z4",),
+        (4, "h5", "g6",),
     ),
     "up": (
-        (0, "z4",),
-        (2, "i5",),
-        (3, "h6", "g7",),
-        (4, "z5",),
-        (6, "i6",),
-        (7, "h7",),
+        (1, "e7", "i5", "f6", "o6",),
+        (3, "z5", "h6", "g7",),
+        (6, "i6", "f7",),
     ),
     "down": (
-        (0, "f7", "i7", "z6",),
+        (0, "z6", "h7", "i7",),
         (1, "z7",),
     ),
     "tail": (
@@ -250,24 +235,44 @@
 }
 
 
+DENOISER = (
+    ((10, 8, 16), jnp.float32),
+    ((512, 512), jnp.float32),
+    ((10, 512), jnp.float32),
+    ((16, 512), jnp.float32),
+    ((3, 512), jnp.float32),
+    ((512, 1536), jnp.bfloat16),
+    ((512, 512), jnp.bfloat16),
+    ((512, 512), jnp.bfloat16),
+    ((512, 1024), jnp.bfloat16),
+    ((512, 512), jnp.bfloat16),
+    ((512, 2048), jnp.bfloat16),
+    ((2048, 512), jnp.bfloat16),
+    ((10, 512), jnp.float32),
+)
+BROUGHT = len(DENOISER) + 4
+
+
+def whole_kernel(*refs):
+    levels_ref = refs[0]
+    given = refs[1 : 10 + len(DENOISER)]
+    actions_ref = refs[10 + len(DENOISER)]
+    rest = refs[11 + len(DENOISER) :]
+    encode_kernel(levels_ref, given, actions_ref, rest[:BROUGHT], rest[BROUGHT : BROUGHT + 10], *rest[BROUGHT + 10 :])
+
+
 def encode_kernel(
-    pixels_ref,
-    patch_ref,
-    position_ref,
-    gains_ref,
-    qkv_ref,
-    out_ref,
-    up_ref,
-    down_ref,
-    cond_ref,
-    result_ref,
+    levels_ref,
+    given,
+    actions_ref,
+    held,
+    denoiser_scratch,
     patch_full,
     qkv_full,
     out_full,
     up_full,
     down_full,
     spread,
-    pixels,
     place,
     state,
     normed,
@@ -281,7 +286,19 @@
     kept,
     slab_sent,
     slab_came,
+    brought,
 ):
+    pixels_in, patch_ref, position_in, gains_in, qkv_ref, out_ref, up_ref, down_ref, cond_in = given[:9]
+    pixels_ref, position_ref, gains_ref, cond_ref = held[:4]
+    pixels = hidden.at[:, 0:768]
+    incoming = (pixels_in, position_in, gains_in, cond_in, *given[9:])
+
+    def bring(i):
+        return pltpu.make_async_copy(incoming[i], held[i], brought.at[i])
+
+    begin, finish = denoiser(
+        levels_ref, landed, *held[4:], actions_ref, *denoiser_scratch
+    )
     batch = lax.axis_index("batch")
     part = lax.axis_index("mp")
     near, y = batch // 4, batch % 4
@@ -476,18 +493,28 @@
     def columns(i, width):
         return pl.ds(pl.multiple_of(i * width, 128), width)
 
-    move(PLAN["prepare"][0][1:])
+    first, second, third = PLAN["prepare"]
+    move(first)
+    for i in range(BROUGHT):
+        bring(i).start()
+    for i in range(BROUGHT):
+        bring(i).wait()
     for part_at in range(6):
         lanes = pl.ds(part_at * 128, 128)
-        spread[part_at] = pixels_ref[:, :, lanes].astype(jnp.float32).reshape(800, 128)
-    for frame in range(FRAMES):
-        pixels[frame * ROWS + 96 : (frame + 1) * ROWS, :] = jnp.zeros((16, 768), jnp.bfloat16)
-        for part_at in range(6):
+        spread[...] = pixels_ref[:, :, lanes].astype(jnp.float32).reshape(800, 128)
+        for frame in range(FRAMES):
+            if part_at == 0:
+                pixels[frame * ROWS + 96 : (frame + 1) * ROWS, :] = jnp.zeros(
+                    (16, 768), jnp.bfloat16
+                )
             pixels[frame * ROWS : frame * ROWS + 100, part_at * 128 : part_at * 128 + 128] = spread[
-                part_at, pl.ds(frame, 100, stride=FRAMES), :
+                pl.ds(frame, 100, stride=FRAMES), :
             ].astype(jnp.bfloat16)
     place[96:ROWS, :] = jnp.zeros((16, 1024), jnp.float32)
     place[0:100, :] = position_ref[...].astype(jnp.float32)
+    move(second)
+    begin()
+    move(third)
 
     def embed(i):
         cols = columns(i, 512)
@@ -578,8 +605,8 @@
             device_id=partner,
             device_id_type=MESH,
         ).wait_recv()
-        result_ref[source] = landed[source]
-    result_ref[batch] = leaving[batch]
+    landed[batch] = leaving[batch]
+    finish()
     for by in range(1, FRAMES):
         slab(by).wait_send()
     for k in range(CHUNKS):
@@ -587,24 +614,37 @@
             copy_out(k, slot).wait_send()
 
 
-def encode(pixels, patch, position, gains, qkv, out, up, down, cond):
+def run_all(levels, *arrays):
     bf16, f32 = jnp.bfloat16, jnp.float32
-    whole = pl.BlockSpec(memory_space=VMEM)
     apart = pl.BlockSpec(memory_space=pl.ANY)
     tall = FRAMES * ROWS
     return pl.pallas_call(
-        encode_kernel,
-        out_shape=jax.ShapeDtypeStruct((FRAMES, KEYS, 512), bf16),
-        in_specs=[whole, apart, whole, whole, apart, apart, apart, apart, whole],
-        out_specs=whole,
+        whole_kernel,
+        out_shape=jax.ShapeDtypeStruct((10, 8, 16), f32),
+        in_specs=[pl.BlockSpec(memory_space=pltpu.SMEM)] + [apart] * len(arrays),
+        out_specs=pl.BlockSpec(memory_space=VMEM),
         scratch_shapes=[
+            VMEM((100, FRAMES, 768), bf16),
+            VMEM((100, 1024), bf16),
+            VMEM((3, 1024), f32),
+            VMEM((1024, 512), bf16),
+            *[VMEM(shape, kind) for shape, kind in DENOISER],
+            VMEM((8 * KEYS, 1024), bf16),
+            VMEM((8, 512), f32),
+            VMEM((128, 1536), bf16),
+            VMEM((128, 512), bf16),
+            VMEM((16, 128), f32),
+            VMEM((128, 16), f32),
+            VMEM((16, 512), f32),
+            VMEM((16, 512), f32),
+            VMEM((512, 16), f32),
+            VMEM((128, 512), f32),
             VMEM((768, 1024), bf16),
             VMEM((1024, 3072), bf16),
             VMEM((1024, 1024), bf16),
             VMEM((1024, 4096), bf16),
             VMEM((4096, 1024), bf16),
-            VMEM((6, 800, 128), f32),
-            VMEM((tall, 768), bf16),
+            VMEM((800, 128), f32),
             VMEM((ROWS, 1024), f32),
             VMEM((tall, 1024), f32),
             VMEM((tall, 1024), bf16),
@@ -618,11 +658,12 @@
             pltpu.SemaphoreType.DMA((CHUNKS,)),
             pltpu.SemaphoreType.DMA((FRAMES,)),
             pltpu.SemaphoreType.DMA((FRAMES,)),
+            pltpu.SemaphoreType.DMA((BROUGHT,)),
         ],
         compiler_params=pltpu.CompilerParams(
             vmem_limit_bytes=67043328, collective_id=0, has_side_effects=True
         ),
-    )(pixels, patch, position, gains, qkv, out, up, down, cond)
+    )(levels, *arrays)
 
 
 def on_device(
@@ -650,7 +691,8 @@
     noise,
     timesteps,
 ):
-    condition = encode(
+    actions = run_all(
+        timesteps,
         jnp.transpose(pixels.reshape(pixels.shape[2:]), (1, 0, 2)),
         patch_weight,
         position,
@@ -660,11 +702,7 @@
         up_weight,
         down_weight,
         cond_weight,
-    )
-    actions = denoise(
-        timesteps,
         jnp.transpose(noise.reshape(noise.shape[2:]), (2, 0, 1)),
-        condition.reshape(FRAMES * KEYS, -1),
         time_weight,
         action_in,
         action_pos,

time: 116 us -> 105 us (0.905)
  Pallas kernels: 116 us -> 103 us
  local copies, waits for them, and re-layouts: 0 us -> 1.4 us
    pallas_call x2 -> x1, Pallas kernels: 116 us -> 103 us  [run_all(): pl.pallas_call(whole_kernel, out_shape=jax.ShapeDtypeStruct((10, 8, 16),...]
    unnamed x0 -> x1, local copies, waits for them, and re-layouts: none -> 1.4 us
where the time goes in v3:
time: 105 us
  Pallas kernels  103 us (98%)
  local copies, waits for them, and re-layouts  1.4 us (1%)
    pallas_call x1, Pallas kernels, run_all(): pl.pallas_call(whole_kernel, out_shape=jax.ShapeDtypeStruct((10, 8, 16),...  103 us

profile of v3, /device:TPU:0, one launch (start us, length us, event | category | flops | bytes accessed | tf_op | source)
XLA Modules:
  0.0 104.7 jit_solution(11132545492525229684)
XLA Ops:
  0.0 103.3 %shard_map.217 = f32[10,8,16]{2,1,0:T(8,128)} custom-call(s32[4]{0:T(128)} %refs_0_.1, bf16[100,8,768]{2,1,0:T(8,128)(2,1)} %bitcast.10, bf16[48,1024]{1,0:T(8,128)(2,1)} %refs_2_.1, bf16[100,1024]{1,0:T(8,128)(2,1)} %refs_3_.1, f32[3,1024]{1,0:T(4,128)} %refs_4_.1, bf16[64,3072]{1,0:T(8,128)(2,1)} %refs_5_.1, bf16[64,1024]{1,0:T(8,128)(2,1)} %refs_6_.1, ...), custom_call_target="tpu_custom_call" | custom-call | tf_op jit(solution)/shard_map/pallas_call | solution.py:621
  103.3 1.4 %copy.25 = f32[1,1,8,16,10]{3,2,4,1,0:T(8,128)} copy(f32[1,1,8,16,10]{3,2,4,1,0:T(8,128)} %bitcast.11) | data formatting | bytes 10240

commit v4 on v3

--- a/solution.py
+++ b/solution.py
@@ -65,7 +65,8 @@
 
 
 def gelu(values):
-    return 0.5 * values * (1.0 + lax.erf(values * math.sqrt(0.5)))
+    small = 0.5 * values
+    return small + small * lax.erf(values * math.sqrt(0.5))
 
 
 def denoiser(
@@ -116,7 +117,10 @@
                 packed[:, 2 * width + at : 2 * width + at + 128],
                 same,
             )
-        held_state[...] = state + product(context[...], self_out_ref[...])
+        state = state + product(context[...], self_out_ref[...])
+        held_state[...] = state
+        normed = normalize(state, gains_ref[1:2, :]).astype(jnp.bfloat16)
+        packed[:, 0:width] = product(normed, query_ref[...]).astype(jnp.bfloat16)
 
     def begin():
         row = lax.broadcasted_iota(jnp.int32, (8, width // 2), 0)
@@ -142,8 +146,6 @@
         held = lax.rem(slot, KEYS) < 25
         sample = sample_now[...]
         state = held_state[...]
-        normed = normalize(state, gains_ref[1:2, :]).astype(jnp.bfloat16)
-        packed[:, 0:width] = product(normed, query_ref[...]).astype(jnp.bfloat16)
         for pair in range(4):
             at = pair * 128
             context[:, at : at + 128] = pair_attention(
@@ -183,52 +185,53 @@
 FRAMES = 8
 ROWS = 112
 LINKS = 24
-CHUNKS = 8
+CHUNKS = 9
 MESH = pl.DeviceIdType.MESH
 PLAN = {
     "prepare": (
-        ("a0", "a1", "o0", "a2", "o1",),
-        ("b0", "c0", "b1", "c1", "o5", "a3", "o7", "d0", "b2", "e0", "c2", "d1", "g0", "a4", "f0", "f1", "o2", "o3", "c3", "e1",),
-        ("h0", "g1", "d2", "i0", "e2", "a5", "b3", "f2", "h1", "z0",),
+        ("a0", "a1", "a3", "a2",),
+        ("o8", "o6", "b0", "o2", "c0", "o0", "b1", "c1", "a4", "b3", "d0", "b2", "o3", "f0", "c2", "c3", "e0", "a5",),
+        ("d1", "g0", "e1", "o1", "d2", "h0", "b4", "e2", "c4", "d3", "i0", "o7", "f1", "g1", "f2", "a6", "z0",),
     ),
     "embed": (
+        (1, "g2", "e3",),
     ),
     "first_norm": (
-        (0, "i1",),
-        (2, "c4",),
-        (3, "g2",),
-        (6, "b4",),
-        (7, "z1", "h2",),
+        (0, "h1", "g3",),
+        (2, "b5", "d4",),
+        (3, "c5", "i1",),
+        (6, "e4",),
+        (7, "h2", "a7", "i2",),
     ),
     "qkv": (
-        (0, "a6", "o4",),
-        (2, "i2", "f3", "e3", "d3", "b5",),
-        (3, "c5", "z2",),
-        (4, "e4",),
-        (5, "d4", "a7", "f4",),
+        (0, "z1", "f3",),
+        (1, "g4", "i3", "b6", "h3", "f4", "z2", "d5",),
+        (2, "f5", "z3", "o4", "a8", "c6", "o5", "e5",),
     ),
     "att": (
-        (0, "g3",),
-        (2, "h3", "d5",),
-        (3, "b6",),
-        (4, "i3", "g4", "f5", "h4", "c6",),
-        (5, "e5",),
-        (7, "d6", "b7", "z3", "c7", "i4", "g5",),
+        (1, "h4", "g5",),
+        (2, "b7", "c7", "d6",),
+        (4, "h5", "i4", "f6", "b8",),
+        (6, "c8", "e6",),
+        (7, "z4", "d7", "i5", "f7", "g6",),
     ),
     "out": (
+        (1, "e7",),
     ),
     "second_norm": (
-        (1, "d7", "e6", "z4",),
-        (4, "h5", "g6",),
+        (0, "d8",),
+        (4, "h6",),
+        (5, "z5",),
     ),
     "up": (
-        (1, "e7", "i5", "f6", "o6",),
-        (3, "z5", "h6", "g7",),
-        (6, "i6", "f7",),
+        (0, "g7", "e8", "i6",),
+        (1, "f8",),
+        (2, "g8", "z6", "h7",),
+        (3, "i7", "h8",),
     ),
     "down": (
-        (0, "z6", "h7", "i7",),
-        (1, "z7",),
+        (0, "z7", "i8",),
+        (1, "z8",),
     ),
     "tail": (
     ),
@@ -320,8 +323,9 @@
 
     chunks = (
         (patch_ref, patch_full, 48, 0, 1024),
-        (qkv_ref, qkv_full, 64, 0, 1536),
-        (qkv_ref, qkv_full, 64, 1536, 1536),
+        (qkv_ref, qkv_full, 64, 0, 1024),
+        (qkv_ref, qkv_full, 64, 1024, 1024),
+        (qkv_ref, qkv_full, 64, 2048, 1024),
         (out_ref, out_full, 64, 0, 1024),
         (up_ref, up_full, 64, 0, 2048),
         (up_ref, up_full, 64, 2048, 2048),
@@ -525,10 +529,10 @@
     run(FRAMES, norm_rows(0), "first_norm")
 
     def pack(i):
-        cols = columns(i, 512)
+        cols = columns(i, 1024)
         packed[:, cols] = product(normed[...], qkv_full[:, cols]).astype(jnp.bfloat16)
 
-    run(6, pack, "qkv")
+    run(3, pack, "qkv")
 
     key_at = lax.broadcasted_iota(jnp.int32, (2 * ROWS, ROWS), 1)
 
@@ -546,17 +550,20 @@
     run(FRAMES, attend, "att")
 
     def project(i):
-        cols = columns(i, 512)
-        state[:, cols] += product(normed[...], out_full[:, cols])
+        rows = pl.ds(pl.multiple_of(i * 448, 16), 448)
+        grown = state[rows, :] + product(normed[rows, :], out_full[...])
+        state[rows, :] = grown
+        normed[rows, :] = normalize(grown, gains_ref[1:2, :]).astype(jnp.bfloat16)
 
     run(2, project, "out")
-    run(FRAMES, norm_rows(1), "second_norm")
+    for _, *names in PLAN["second_norm"]:
+        move(names)
 
     def grow(i):
-        cols = columns(i, 512)
+        cols = columns(i, 1024)
         hidden[:, cols] = gelu(product(normed[...], up_full[:, cols])).astype(jnp.bfloat16)
 
-    run(8, grow, "up")
+    run(4, grow, "up")
 
     def shrink(i):
         cols = columns(i, 512)
@@ -595,6 +602,10 @@
 
     for by in range(1, FRAMES):
         slab(by).start()
+    for k in range(CHUNKS):
+        for slot in range(LINKS):
+            copy_out(k, slot).wait_send()
+    landed[batch] = leaving[batch]
     for by in range(1, FRAMES):
         source = (batch + FRAMES - by) % FRAMES
         pltpu.make_async_remote_copy(
@@ -605,13 +616,9 @@
             device_id=partner,
             device_id_type=MESH,
         ).wait_recv()
-    landed[batch] = leaving[batch]
     finish()
     for by in range(1, FRAMES):
         slab(by).wait_send()
-    for k in range(CHUNKS):
-        for slot in range(LINKS):
-            copy_out(k, slot).wait_send()
 
 
 def run_all(levels, *arrays):

time: 105 us -> 104 us (level)
    pallas_call x1, Pallas kernels: 103 us -> 102 us  [run_all(): pl.pallas_call(whole_kernel, out_shape=jax.ShapeDtypeStruct((10, 8, 16),...]
where the time goes in v4:
time: 104 us
  Pallas kernels  102 us (98%)
  local copies, waits for them, and re-layouts  1.4 us (1%)
    pallas_call x1, Pallas kernels, run_all(): pl.pallas_call(whole_kernel, out_shape=jax.ShapeDtypeStruct((10, 8, 16),...  102 us

profile of v4, /device:TPU:0, one launch (start us, length us, event | category | flops | bytes accessed | tf_op | source)
XLA Modules:
  0.0 103.6 jit_solution(6592443150399945397)
XLA Ops:
  0.0 102.2 %shard_map.217 = f32[10,8,16]{2,1,0:T(8,128)} custom-call(s32[4]{0:T(128)} %refs_0_.1, bf16[100,8,768]{2,1,0:T(8,128)(2,1)} %bitcast.10, bf16[48,1024]{1,0:T(8,128)(2,1)} %refs_2_.1, bf16[100,1024]{1,0:T(8,128)(2,1)} %refs_3_.1, f32[3,1024]{1,0:T(4,128)} %refs_4_.1, bf16[64,3072]{1,0:T(8,128)(2,1)} %refs_5_.1, bf16[64,1024]{1,0:T(8,128)(2,1)} %refs_6_.1, ...), custom_call_target="tpu_custom_call" | custom-call | tf_op jit(solution)/shard_map/pallas_call | solution.py:628
  102.2 1.4 %copy.25 = f32[1,1,8,16,10]{3,2,4,1,0:T(8,128)} copy(f32[1,1,8,16,10]{3,2,4,1,0:T(8,128)} %bitcast.11) | data formatting | bytes 10240

commit v5 on v4

--- a/solution.py
+++ b/solution.py
@@ -135,9 +135,9 @@
             widened[8:16, :] = jnp.zeros((8, width), jnp.float32)
             widened[0:10, :] = given[...]
         out_columns[...] = widened_out[...].T
-        flat[...] = jnp.zeros_like(flat)
+        number = lax.broadcasted_iota(jnp.int32, (16, 16), 0)
         for cand in range(8):
-            flat[0:10, cand * 16 : cand * 16 + 16] = noise_ref[:, cand, :]
+            flat[:, cand * 16 : cand * 16 + 16] = jnp.where(number < 10, noise_ref[:, cand, :], 0.0)
         sample_now[...] = flat[...].T
         first_half(0)
 
@@ -177,7 +177,8 @@
         lax.fori_loop(0, STEPS, one_step, 0)
         flat[...] = sample_now[...].T
         for cand in range(8):
-            actions_ref[:, cand, :] = flat[0:10, cand * 16 : cand * 16 + 16]
+            noise_ref[:, cand, :] = flat[:, cand * 16 : cand * 16 + 16]
+        actions_ref[...] = noise_ref[0:10]
 
     return begin, finish
 
@@ -239,7 +240,7 @@
 
 
 DENOISER = (
-    ((10, 8, 16), jnp.float32),
+    ((16, 8, 16), jnp.float32),
     ((512, 512), jnp.float32),
     ((10, 512), jnp.float32),
     ((16, 512), jnp.float32),
@@ -297,7 +298,8 @@
     incoming = (pixels_in, position_in, gains_in, cond_in, *given[9:])
 
     def bring(i):
-        return pltpu.make_async_copy(incoming[i], held[i], brought.at[i])
+        target = held[i].at[0:10] if i == 4 else held[i]
+        return pltpu.make_async_copy(incoming[i], target, brought.at[i])
 
     begin, finish = denoiser(
         levels_ref, landed, *held[4:], actions_ref, *denoiser_scratch
@@ -505,7 +507,7 @@
         bring(i).wait()
     for part_at in range(6):
         lanes = pl.ds(part_at * 128, 128)
-        spread[...] = pixels_ref[:, :, lanes].astype(jnp.float32).reshape(800, 128)
+        spread[0:800, :] = pixels_ref[:, :, lanes].astype(jnp.float32).reshape(800, 128)
         for frame in range(FRAMES):
             if part_at == 0:
                 pixels[frame * ROWS + 96 : (frame + 1) * ROWS, :] = jnp.zeros(
@@ -651,7 +653,7 @@
             VMEM((1024, 1024), bf16),
             VMEM((1024, 4096), bf16),
             VMEM((4096, 1024), bf16),
-            VMEM((800, 128), f32),
+            VMEM((832, 128), f32),
             VMEM((ROWS, 1024), f32),
             VMEM((tall, 1024), f32),
             VMEM((tall, 1024), bf16),

time: 104 us -> 104 us (level)
  no operation moved by 1% of the time
where the time goes in v5:
time: 104 us
  Pallas kernels  102 us (98%)
  local copies, waits for them, and re-layouts  1.4 us (1%)
    pallas_call x1, Pallas kernels, run_all(): pl.pallas_call(whole_kernel, out_shape=jax.ShapeDtypeStruct((10, 8, 16),...  102 us

profile of v5, /device:TPU:0, one launch (start us, length us, event | category | flops | bytes accessed | tf_op | source)
XLA Modules:
  0.0 103.6 jit_solution(3289026939952717641)
XLA Ops:
  0.0 102.2 %shard_map.217 = f32[10,8,16]{2,1,0:T(8,128)} custom-call(s32[4]{0:T(128)} %refs_0_.1, bf16[100,8,768]{2,1,0:T(8,128)(2,1)} %bitcast.10, bf16[48,1024]{1,0:T(8,128)(2,1)} %refs_2_.1, bf16[100,1024]{1,0:T(8,128)(2,1)} %refs_3_.1, f32[3,1024]{1,0:T(4,128)} %refs_4_.1, bf16[64,3072]{1,0:T(8,128)(2,1)} %refs_5_.1, bf16[64,1024]{1,0:T(8,128)(2,1)} %refs_6_.1, ...), custom_call_target="tpu_custom_call" | custom-call | tf_op jit(solution)/shard_map/pallas_call | solution.py:630
  102.2 1.4 %copy.25 = f32[1,1,8,16,10]{3,2,4,1,0:T(8,128)} copy(f32[1,1,8,16,10]{3,2,4,1,0:T(8,128)} %bitcast.11) | data formatting | bytes 10240
